TPU v7x, 32 devices: a whole 2x2x4 slice. The times are simulated.
32 devices in a mesh: shard: 2 (over core), ctx: 4 (over y, x), tensor: 4 (over z).
Axes of the slice: x: 2, y: 2, z: 4, core: 2. Of those that a mesh axis runs over, the one named last changes fastest.
Arguments:
- block_input: bfloat16 [4, 2048, 1536], P('shard', 'ctx', 'tensor'), may hold values from -6 to 6
- output_cotangent: bfloat16 [4, 2048, 1536], P('shard', 'ctx', 'tensor'), may hold values from -6 to 6
- norm_gain: bfloat16 [1536], P(('shard', 'ctx')), may hold values from 0.099609375 to 1.8984375
- gate_value_weight: bfloat16 [1536, 2, 3072], P(('shard', 'ctx'), None, 'tensor'), may hold values from -0.15625 to 0.15625
- matrix_weight: bfloat16 [1536, 256], P(('shard', 'ctx')), may hold values from -0.15625 to 0.15625
- step_weight: bfloat16 [1536, 48], P(('shard', 'ctx'), 'tensor'), may hold values from -0.15625 to 0.15625
- out_weight: bfloat16 [1536, 3072], P(('shard', 'ctx'), 'tensor'), may hold values from -0.109375 to 0.109375
- value_kernel: float32 [4, 3072], P(None, 'tensor'), may hold values from -3 to 3
- value_bias: float32 [3072], P('tensor'), may hold values from -3 to 3
- matrix_kernel: float32 [4, 256], replicated, may hold values from -3 to 3
- matrix_bias: float32 [256], replicated, may hold values from -3 to 3
- step_bias: float32 [48], P('tensor'), may hold values from -7 to -3
- decay_log: float32 [48], P('tensor'), may hold values from -4 to 1
- skip_gain: float32 [48], P('tensor'), may hold values from 0.5 to 1.5
- inner_gain: float32 [3072], P('tensor'), may hold values from 0.1 to 1.9
Outputs:
- block_output: bfloat16 [4, 2048, 1536], P('shard', 'ctx', 'tensor')
- input_grad: float32 [4, 2048, 1536], P('shard', 'ctx', 'tensor')
- norm_gain_grad: float32 [1536], P(('shard', 'ctx'))
- gate_value_grad: float32 [1536, 2, 3072], P(('shard', 'ctx'), None, 'tensor')
- matrix_weight_grad: float32 [1536, 256], P(('shard', 'ctx'))
- step_weight_grad: float32 [1536, 48], P(('shard', 'ctx'), 'tensor')
- out_weight_grad: float32 [1536, 3072], P(('shard', 'ctx'), 'tensor')
- value_kernel_grad: float32 [4, 3072], P(None, 'tensor')
- value_bias_grad: float32 [3072], P('tensor')
- matrix_kernel_grad: float32 [4, 256], replicated
- matrix_bias_grad: float32 [256], replicated
- step_bias_grad: float32 [48], P('tensor')
- decay_log_grad: float32 [48], P('tensor')
- skip_gain_grad: float32 [48], P('tensor')
- inner_gain_grad: float32 [3072], P('tensor')
All inputs are finite; a program needn't handle non-finite values.
Results may differ from a plain program's by a relative error of at most 0.012.
Values may be sent and summed in bfloat16 or wider, within the bound.
A program may use at most 192 MiB of HBM per device.

v0:
```python
import jax
import jax.numpy as jnp
from jax import lax
from jax.sharding import PartitionSpec as P

BLOCK = 256


HIGHEST = lax.Precision.HIGHEST
EPSILON = 1e-05


def passed_along(block, axis, distance):
    devices = range(lax.axis_size(axis))
    route = [(i - distance, i) for i in devices if i - distance in devices]
    return lax.ppermute(block, axis, route)


def entering(value, axis, join, neutral, backward):
    count, mine = (lax.axis_size(axis), lax.axis_index(axis))
    pieces = jax.tree.map(lambda part: lax.all_gather(part, axis), value)
    if backward:
        pieces = jax.tree.map(lambda part: part[::-1], pieces)
        mine = count - 1 - mine
    so_far = jax.tree.map(
        lambda part, zero: jnp.full_like(part, 0) + jnp.asarray(zero, part.dtype), value, neutral
    )

    def hop(position, so_far):
        longer = join(so_far, jax.tree.map(lambda part: part[position], pieces))
        return jax.tree.map(lambda new, old: jnp.where(position < mine, new, old), longer, so_far)

    return lax.fori_loop(0, count - 1, hop, so_far)


def silu_slope(value):
    sigma = jax.nn.sigmoid(value)
    return sigma * (1.0 + value * (1.0 - sigma))


def dot_rows(left, right):
    return lax.dot_general(
        left, right, (((1,), (1,)), ((), ())), preferred_element_type=jnp.float32
    )


def dot_tokens(left, right):
    return lax.dot_general(
        left, right, (((0,), (0,)), ((), ())), preferred_element_type=jnp.float32
    )


def causal_conv(signal, before, kernel, bias):
    kernel_width = kernel.shape[0]
    seq_rows = signal.shape[-2]
    padded = jnp.concatenate([before, signal], axis=-2)
    total = jnp.zeros_like(signal) + bias
    for offset in range(kernel_width):
        total = total + kernel[offset] * padded[..., offset : offset + seq_rows, :]
    return total


def conv_transpose(grad, after, kernel):
    kernel_width = kernel.shape[0]
    seq_rows = grad.shape[-2]
    padded = jnp.concatenate([grad, after], axis=-2)
    total = jnp.zeros_like(grad)
    for offset in range(kernel_width):
        first = kernel_width - 1 - offset
        total = total + kernel[offset] * padded[..., first : first + seq_rows, :]
    return total


def kernel_grad(grad, signal, before):
    kernel_width = before.shape[-2] + 1
    seq_rows = grad.shape[-2]
    padded = jnp.concatenate([before, signal], axis=-2)
    summed_axes = tuple(range(grad.ndim - 1))
    return jnp.stack(
        [
            jnp.sum(grad * padded[..., offset : offset + seq_rows, :], axis=summed_axes)
            for offset in range(kernel_width)
        ]
    )


def decay_matrix(cum_decay):
    by_head = cum_decay.T
    spread = by_head[:, :, None] - by_head[:, None, :]
    token_count = cum_decay.shape[0]
    causal = (jnp.arange(token_count)[:, None] >= jnp.arange(token_count)[None, :])[None]
    return jnp.where(causal, jnp.exp(jnp.where(causal, spread, 0.0)), 0.0)


def block_forward(values, b_matrix, c_matrix, log_decay, step_size, start):
    cum_decay = jnp.cumsum(log_decay, axis=0)
    weights = decay_matrix(cum_decay) * jnp.dot(c_matrix, b_matrix.T, precision=HIGHEST)[None]
    scaled = values * step_size[:, :, None]
    inside = jnp.einsum("hts,shp->thp", weights, scaled, precision=HIGHEST)
    carried = jnp.exp(cum_decay)[:, :, None] * jnp.einsum(
        "tn,hnp->thp", c_matrix, start, precision=HIGHEST
    )
    to_end = jnp.exp(cum_decay[-1][None, :] - cum_decay)
    final_state = jnp.exp(cum_decay[-1])[:, None, None] * start + jnp.einsum(
        "sn,shp->hnp", b_matrix, scaled * to_end[:, :, None], precision=HIGHEST
    )
    return (inside + carried, final_state)


def block_backward(
    values, b_matrix, c_matrix, log_decay, step_size, start, ssd_part, grad_part, incoming
):
    cum_decay = jnp.cumsum(log_decay, axis=0)
    decays = decay_matrix(cum_decay)
    weights = decays * jnp.dot(c_matrix, b_matrix.T, precision=HIGHEST)[None]
    to_end = jnp.exp(cum_decay[-1][None, :] - cum_decay)
    from_start = jnp.exp(cum_decay)
    b_dot = jnp.einsum("hts,thp->shp", weights, grad_part, precision=HIGHEST) + to_end[
        :, :, None
    ] * jnp.einsum("sn,hnp->shp", b_matrix, incoming, precision=HIGHEST)
    pair_dots = jnp.einsum("thp,shp->hts", grad_part, values, precision=HIGHEST)
    mixing = jnp.einsum("hts,sh->ts", decays * pair_dots, step_size, precision=HIGHEST)
    grad_b = jnp.dot(mixing.T, c_matrix, precision=HIGHEST) + jnp.einsum(
        "shp,hnp->sn", values * (step_size * to_end)[:, :, None], incoming, precision=HIGHEST
    )
    weighted_grad = grad_part * from_start[:, :, None]
    grad_c = jnp.dot(mixing, b_matrix, precision=HIGHEST) + jnp.einsum(
        "thp,hnp->tn", weighted_grad, start, precision=HIGHEST
    )
    earlier = jnp.exp(cum_decay[-1])[:, None, None] * incoming + jnp.einsum(
        "tn,thp->hnp", c_matrix, weighted_grad, precision=HIGHEST
    )
    value_dot = jnp.sum(values * b_dot, axis=2)
    cum_grad = jnp.sum(grad_part * ssd_part, axis=2) - step_size * value_dot
    return (earlier, (b_dot, grad_b, grad_c, value_dot, cum_grad))


def run_forward(values, b_matrix, c_matrix, log_decay, step_size, start):
    seq_rows = values.shape[0]
    block_count = seq_rows // BLOCK

    def blocks(array):
        return array.reshape((block_count, BLOCK) + array.shape[1:])

    def advance(current, pieces):
        output, final_state = block_forward(*pieces, current)
        return (final_state, (output, current))

    unused, (outputs, starts) = lax.scan(
        advance,
        start,
        (blocks(values), blocks(b_matrix), blocks(c_matrix), blocks(log_decay), blocks(step_size)),
    )
    return (outputs.reshape(values.shape), starts)


def run_backward(
    values, b_matrix, c_matrix, log_decay, step_size, starts, ssd_out, grad_mixed, incoming
):
    seq_rows = values.shape[0]
    block_count = seq_rows // BLOCK

    def blocks(array):
        return array.reshape((block_count, BLOCK) + array.shape[1:])

    def retreat(current, pieces):
        return block_backward(*pieces, current)

    unused, results = lax.scan(
        retreat,
        incoming,
        (
            blocks(values),
            blocks(b_matrix),
            blocks(c_matrix),
            blocks(log_decay),
            blocks(step_size),
            starts,
            blocks(ssd_out),
            blocks(grad_mixed),
        ),
        reverse=True,
    )
    return tuple((item.reshape((seq_rows,) + item.shape[2:]) for item in results))


def chain_link(first_part, second_part):
    return (
        first_part[0] * second_part[0],
        second_part[0][:, :, None, None] * first_part[1] + second_part[1],
    )


def body(
    block_input,
    output_cotangent,
    norm_gain,
    gate_value_weight,
    matrix_weight,
    step_weight,
    out_weight,
    value_kernel,
    value_bias,
    matrix_kernel,
    matrix_bias,
    step_bias,
    decay_log,
    skip_gain,
    inner_gain,
):
    sequences, seq_length, quarter = block_input.shape
    head_count = step_bias.shape[0]
    inner_width = inner_gain.shape[0]
    head_width = inner_width // head_count
    state_width = matrix_weight.shape[1] // 2
    kernel_width = value_kernel.shape[0]
    row_count = sequences * seq_length
    tensor_count = lax.axis_size("tensor")
    inner_total = inner_width * tensor_count
    feature_start = lax.axis_index("tensor") * quarter
    full_input, full_cot = (
        lax.all_gather(block_input, "tensor", axis=2, tiled=True),
        lax.all_gather(output_cotangent, "tensor", axis=2, tiled=True),
    )
    model_width = full_input.shape[2]
    gathered = (
        lax.all_gather(norm_gain, ("shard", "ctx"), axis=0, tiled=True),
        lax.all_gather(gate_value_weight, ("shard", "ctx"), axis=0, tiled=True),
        lax.all_gather(matrix_weight, ("shard", "ctx"), axis=0, tiled=True),
        lax.all_gather(step_weight, ("shard", "ctx"), axis=0, tiled=True),
        lax.all_gather(out_weight, ("shard", "ctx"), axis=0, tiled=True),
    )
    gain_all, gate_value_all, matrix_all, step_all, out_all = gathered
    inputs = full_input.reshape(row_count, model_width).astype(jnp.float32)
    input_scale = lax.rsqrt(jnp.mean(inputs * inputs, axis=1, keepdims=True) + EPSILON)
    normalized = inputs * input_scale
    gain_float = gain_all.astype(jnp.float32)
    normed = (normalized * gain_float[None, :]).astype(jnp.bfloat16)
    gate_value = lax.optimization_barrier(
        jnp.dot(
            normed,
            gate_value_all.reshape(model_width, 2 * inner_width),
            preferred_element_type=jnp.float32,
        ).astype(jnp.bfloat16)
    )
    matrix_low = lax.optimization_barrier(
        jnp.dot(normed, matrix_all, preferred_element_type=jnp.float32).astype(jnp.bfloat16)
    )
    step_raw = jnp.dot(normed, step_all, preferred_element_type=jnp.float32).reshape(
        sequences, seq_length, head_count
    )
    values_low = gate_value[:, inner_width:].reshape(sequences, seq_length, inner_width)
    matrix_seq = matrix_low.reshape(sequences, seq_length, 2 * state_width)
    tail_rows = jnp.concatenate(
        [
            values_low[:, seq_length - kernel_width + 1 :],
            matrix_seq[:, seq_length - kernel_width + 1 :],
        ],
        axis=2,
    )
    before = passed_along(tail_rows, "ctx", 1).astype(jnp.float32)
    before_values = before[:, :, :inner_width]
    before_matrix = before[:, :, inner_width:]
    values_in = values_low.astype(jnp.float32)
    matrix_in = matrix_seq.astype(jnp.float32)
    gate = gate_value[:, :inner_width].astype(jnp.float32)
    value_conv = causal_conv(values_in, before_values, value_kernel, value_bias)
    values = jax.nn.silu(value_conv)
    matrix_conv = causal_conv(matrix_in, before_matrix, matrix_kernel, matrix_bias)
    matrices = jax.nn.silu(matrix_conv)
    b_matrix = matrices[:, :, :state_width]
    c_matrix = matrices[:, :, state_width:]
    step_size = jax.nn.softplus(step_raw + step_bias)
    rate = -jnp.exp(decay_log)
    log_decay = step_size * rate
    value_heads = values.reshape(sequences, seq_length, head_count, head_width)
    cum_decay = jnp.cumsum(log_decay, axis=1)
    device_decay = cum_decay[:, -1]
    to_end = jnp.exp(device_decay[:, None, :] - cum_decay)
    own_state = jnp.einsum(
        "asn,ashp->ahnp", b_matrix, value_heads * (step_size * to_end)[..., None], precision=HIGHEST
    )
    identity = (jnp.ones_like(device_decay), jnp.zeros_like(own_state))
    start_state = entering((jnp.exp(device_decay), own_state), "ctx", chain_link, identity, False)[
        1
    ]
    ssd_out, starts = jax.vmap(run_forward)(
        value_heads, b_matrix, c_matrix, log_decay, step_size, start_state
    )
    mixed = (ssd_out + skip_gain[:, None] * value_heads).reshape(row_count, inner_width)
    gate_act = jax.nn.silu(gate)
    gated = mixed * gate_act
    square = lax.psum(jnp.sum(gated * gated, axis=1), "tensor")
    inner_scale = lax.rsqrt(square / inner_total + EPSILON)[:, None]
    normed_inner = (gated * inner_scale * inner_gain[None, :]).astype(jnp.bfloat16)
    partial_value = dot_rows(normed_inner, out_all).reshape(sequences, seq_length, model_width)
    share = lax.psum_scatter(partial_value, "tensor", scatter_dimension=2, tiled=True)
    block_output = (block_input.astype(jnp.float32) + share).astype(jnp.bfloat16)
    cot_rows = full_cot.reshape(row_count, model_width)
    grad_inner = jnp.dot(cot_rows, out_all, preferred_element_type=jnp.float32)
    out_grad = dot_tokens(cot_rows, normed_inner)
    inner_gain_grad = jnp.sum(grad_inner * gated * inner_scale, axis=0)
    scaled_grad = grad_inner * inner_gain[None, :]
    row_dot = lax.psum(jnp.sum(scaled_grad * gated, axis=1), "tensor")[:, None] / inner_total
    grad_gated = inner_scale * scaled_grad - gated * inner_scale**3 * row_dot
    grad_mixed = (grad_gated * gate_act).reshape(sequences, seq_length, head_count, head_width)
    grad_gate = grad_gated * mixed * silu_slope(gate)
    skip_grad = jnp.sum(grad_mixed * value_heads, axis=(0, 1, 3))
    own_adjoint = jnp.einsum(
        "asn,ashp->ahnp", c_matrix, grad_mixed * jnp.exp(cum_decay)[..., None], precision=HIGHEST
    )
    incoming = entering((jnp.exp(device_decay), own_adjoint), "ctx", chain_link, identity, True)[1]
    log_start = jnp.sum(
        (own_adjoint + jnp.exp(device_decay)[:, :, None, None] * incoming) * start_state,
        axis=(2, 3),
    )
    b_dot, grad_b, grad_c, value_dot, cum_grad = jax.vmap(run_backward)(
        value_heads, b_matrix, c_matrix, log_decay, step_size, starts, ssd_out, grad_mixed, incoming
    )
    grad_log = log_start[:, None, :] - (jnp.cumsum(cum_grad, axis=1) - cum_grad)
    grad_values = (step_size[..., None] * b_dot + skip_gain[:, None] * grad_mixed).reshape(
        sequences, seq_length, inner_width
    )
    grad_step = value_dot + grad_log * rate
    decay_grad = rate * jnp.sum(grad_log * step_size, axis=(0, 1))
    grad_raw = grad_step * jax.nn.sigmoid(step_raw + step_bias)
    step_bias_grad = jnp.sum(grad_raw, axis=(0, 1))
    summed_matrix = lax.psum(jnp.concatenate([grad_b, grad_c], axis=2), "tensor")
    grad_value_conv = grad_values * silu_slope(value_conv)
    grad_matrix_conv = summed_matrix * silu_slope(matrix_conv)
    edge_rows = jnp.concatenate(
        [grad_value_conv[:, : kernel_width - 1], grad_matrix_conv[:, : kernel_width - 1]], axis=2
    )
    after = passed_along(edge_rows, "ctx", -1)
    grad_values_in = conv_transpose(grad_value_conv, after[:, :, :inner_width], value_kernel)
    grad_matrix_in = conv_transpose(grad_matrix_conv, after[:, :, inner_width:], matrix_kernel)
    value_kernel_grad = kernel_grad(grad_value_conv, values_in, before_values)
    value_bias_grad = jnp.sum(grad_value_conv, axis=(0, 1))
    matrix_kernel_grad = kernel_grad(grad_matrix_conv, matrix_in, before_matrix)
    matrix_bias_grad = jnp.sum(grad_matrix_conv, axis=(0, 1))
    grad_gate_value = jnp.concatenate(
        [grad_gate, grad_values_in.reshape(row_count, inner_width)], axis=1
    ).astype(jnp.bfloat16)
    grad_matrix_low = grad_matrix_in.reshape(row_count, 2 * state_width).astype(jnp.bfloat16)
    grad_raw_low = grad_raw.reshape(row_count, head_count).astype(jnp.bfloat16)
    local_part = dot_rows(
        grad_gate_value, gate_value_all.reshape(model_width, 2 * inner_width)
    ) + dot_rows(grad_raw_low, step_all)
    matrix_part = dot_rows(grad_matrix_low, matrix_all)
    gate_value_grad = dot_tokens(normed, grad_gate_value).reshape(model_width, 2, inner_width)
    matrix_grad = dot_tokens(normed, grad_matrix_low)
    step_grad = dot_tokens(normed, grad_raw_low)
    gain_normal = normalized * gain_float[None, :]
    row_tile = jnp.broadcast_to(
        jnp.sum(local_part * gain_normal, axis=1)[:, None], (row_count, tensor_count)
    )
    norm_tile = jnp.broadcast_to(
        jnp.sum(local_part * normalized, axis=0)[:, None], (model_width, tensor_count)
    )
    part_share, row_summed, norm_summed = (
        lax.psum_scatter(local_part, "tensor", scatter_dimension=1, tiled=True),
        lax.psum_scatter(row_tile, "tensor", scatter_dimension=1, tiled=True),
        lax.psum_scatter(norm_tile, "tensor", scatter_dimension=1, tiled=True),
    )
    row_total = row_summed[:, 0] + jnp.sum(matrix_part * gain_normal, axis=1)
    norm_grad = norm_summed[:, 0] + jnp.sum(matrix_part * normalized, axis=0)
    grad_quarter = part_share + lax.dynamic_slice_in_dim(
        matrix_part, feature_start, quarter, axis=1
    )
    hat_quarter = (
        grad_quarter * lax.dynamic_slice_in_dim(gain_float, feature_start, quarter, axis=0)[None, :]
    )
    normal_quarter = lax.dynamic_slice_in_dim(normalized, feature_start, quarter, axis=1)
    own_grad = (
        input_scale * (hat_quarter - normal_quarter * (row_total[:, None] / model_width))
    ).reshape(sequences, seq_length, quarter)
    input_grad = own_grad + output_cotangent.astype(jnp.float32)
    large_grads = (
        lax.psum_scatter(norm_grad, ("shard", "ctx"), scatter_dimension=0, tiled=True),
        lax.psum_scatter(gate_value_grad, ("shard", "ctx"), scatter_dimension=0, tiled=True),
        lax.psum_scatter(matrix_grad, ("shard", "ctx"), scatter_dimension=0, tiled=True),
        lax.psum_scatter(step_grad, ("shard", "ctx"), scatter_dimension=0, tiled=True),
        lax.psum_scatter(out_grad, ("shard", "ctx"), scatter_dimension=0, tiled=True),
    )
    small_grads = lax.psum(
        (
            value_kernel_grad,
            value_bias_grad,
            matrix_kernel_grad,
            matrix_bias_grad,
            step_bias_grad,
            decay_grad,
            skip_grad,
            inner_gain_grad,
        ),
        ("shard", "ctx"),
    )
    return (block_output, input_grad) + tuple(large_grads) + tuple(small_grads)


def solution(mesh):
    placed = (
        P("shard", "ctx", "tensor"),
        P("shard", "ctx", "tensor"),
        P(("shard", "ctx")),
        P(("shard", "ctx"), None, "tensor"),
        P(("shard", "ctx"), None),
        P(("shard", "ctx"), "tensor"),
        P(("shard", "ctx"), "tensor"),
        P(None, "tensor"),
        P("tensor"),
        P(),
        P(),
        P("tensor"),
        P("tensor"),
        P("tensor"),
        P("tensor"),
    )
    return jax.shard_map(
        body,
        mesh=mesh,
        in_specs=placed,
        out_specs=(
            P("shard", "ctx", "tensor"),
            P("shard", "ctx", "tensor"),
            P(("shard", "ctx")),
            P(("shard", "ctx"), None, "tensor"),
            P(("shard", "ctx"), None),
            P(("shard", "ctx"), "tensor"),
            P(("shard", "ctx"), "tensor"),
            P(None, "tensor"),
            P("tensor"),
            P(),
            P(),
            P("tensor"),
            P("tensor"),
            P("tensor"),
            P("tensor"),
        ),
        check_vma=False,
    )
```

profile of v0, /device:TPU:0, one launch (start us, length us, event | category | flops | bytes accessed | tf_op | source)
XLA Modules:
  0.0 991.6 jit_solution(13426044934148176788)
XLA Ops:
  11.6 15.9 %all-reduce = bf16[1536]{0:T(1024)(128)(2,1)S(1)} all-reduce(bf16[1536]{0:T(1024)(128)(2,1)S(1)} %dynamic-update-slice), channel_id=1, replica_groups=mesh['shard'=2,'ctx'=4,'tensor'=4] {'shard','ctx'}, use_global_device_ids=true, to_apply=%add | all-reduce | flops 1536 | bytes 6144
  28.0 24.4 %all-gather.3 = bf16[8,192,12]{1,2,0:T(8,128)(2,1)S(1)} all-gather(bf16[1,192,12]{1,2,0:T(8,128)(2,1)} %bitcast.551), channel_id=1, replica_groups=mesh['shard'=2,'ctx'=4,'tensor'=4] {'shard','ctx'}, dimensions={0}, use_global_device_ids=true | all-gather | bytes 41472 | tf_op jit(solution)/shard_map/all_gather | solution.py:230
  55.0 28.6 %all_gather.44 = bf16[1536,256]{1,0:T(8,128)(2,1)} all-gather(bf16[192,256]{1,0:T(8,128)(2,1)} %param.27), channel_id=1, replica_groups=mesh['shard'=2,'ctx'=4,'tensor'=4] {'shard','ctx'}, dimensions={0}, use_global_device_ids=true | all-gather | bytes 884736 | tf_op jit(solution)/shard_map/all_gather | solution.py:229
  107.0 7.8 all-gather.13.cloned.1.call-done
  131.2 7.9 fusion.128
  152.1 9.5 all-gather
  173.5 22.7 %all-gather.19.cloned.1.call-done = f32[8,12,128,64]{2,3,1,0:T(8,128)} async-done(((f32[2,12,128,64]{2,3,1,0:T(8,128)}), f32[8,12,128,64]{2,3,1,0:T(8,128)}) %all-gather.19.cloned.1.call-update) | async-done | bytes 3145744 | tf_op jit(solution)/shard_map/all_gather | solution.py:21
  196.2 24.0 %while.68 = (s32[]{:T(128)}, f32[2,12,128,64]{3,2,1,0:T(8,128)}, s32[]{:T(128)}, f32[4,2,12]{2,1,0:T(2,128)S(1)}, f32[4,2,12,128,64]{3,4,2,1,0:T(8,128)}, /*index=5*/s32[]{:T(128)}, s32[]{:T(128)}) while((s32[]{:T(128)}, f32[2,12,128,64]{3,2,1,0:T(8,128)}, s32[]{:T(128)}, f32[4,2,12]{2,1,0:T(2,128)S(1)}, ...), condition=%wide.region_4.5_spmd.clone, body=%wide.region_3.4_spmd.clone.sunk | while | flops 786436 | bytes 5505425 | solution.py:33
  227.0 45.0 %while.66 = (s32[]{:T(128)}, f32[2,12,128,64]{2,3,1,0:T(8,128)}, f32[2,2,256,12,64]{2,4,3,1,0:T(8,128)}, f32[2,2,12,128,64]{3,4,2,1,0:T(8,128)}, f32[2,2,256,12]...) while((s32[]{:T(128)}, f32[2,12,128,64]{2,3,1,0:T(8,128)}, ...), condition=%wide.region_8.9_spmd, body=%wide.region_5.8_spmd.sunk | while | flops 2626754560 | bytes 44202492 | solution.py:149
  239.5 8.5 bitcast_dynamic-update-slice_fusion.7
  261.9 8.5 bitcast_dynamic-update-slice_fusion.7
  293.6 11.7 %psum.77 = f32[1024]{0:T(1024)S(1)} all-reduce(f32[1024]{0:T(1024)S(1)} %get-tuple-element.973), channel_id=1, replica_groups=mesh['shard'=2,'ctx'=4,'tensor'=4] {'tensor'}, use_global_device_ids=true, to_apply=%region_10.11 | all-reduce | flops 1024 | bytes 8192 | tf_op jit(solution)/shard_map/psum | solution.py:293
  305.4 8.6 multiply_reduce_fusion.6
  314.0 8.3 psum.78
  322.3 8.5 fusion.123
  353.9 36.6 %all-gather.21.cloned.1.call-done = f32[8,12,128,64]{2,3,1,0:T(8,128)} async-done(((f32[2,12,128,64]{2,3,1,0:T(8,128)}), f32[8,12,128,64]{2,3,1,0:T(8,128)}) %all-gather.21.cloned.1.call-update) | async-done | bytes 3145744 | tf_op jit(solution)/shard_map/all_gather | solution.py:21
  402.5 9.4 while.69
  420.5 62.0 %while.67 = (s32[]{:T(128)}, f32[2,12,128,64]{2,3,1,0:T(8,128)}, f32[2,2,256,12,64]{2,4,3,1,0:T(8,128)}, f32[2,2,256,128]{3,2,1,0:T(8,128)}, f32[2,2,256,128]{3,...) while((s32[]{:T(128)}, f32[2,12,128,64]{2,3,1,0:T(8,128)}, ...), condition=%wide.region_21.22_spmd, body=%wide.region_16.21_spmd.sunk | while | flops 5456343040 | bytes 111860560 | solution.py:169
  439.0 7.3 multiply_reduce_fusion.20
  469.7 7.3 multiply_reduce_fusion.20
  499.0 7.9 fusion.170
  529.3 10.6 %fusion.171 = (f32[768]{0:T(1024)S(1)}, f32[768]{0:T(1024)}, f32[768]{0:T(1024)}, f32[768]{0:T(1024)}, f32[768]{0:T(1024)S(1)}, /*index=5*/f32[2,512,768]{2,1,0:T(8,128)S(1)}) fusion(bf16[1024,1536]{1,0:T(8,128)(2,1)} %copy-done.23, f32[2,512,768]{2,1,0:T(8,128)} %get-tuple-element.992, f32[2,3,768]{2,1,0:T(4,128)S(1)} %copy-done.46, ...), kind=kLoop, calls=%fused_computation.285 | loop fusion | flops 18870528 | bytes 20484096 | tf_op jit(solution)/shard_map/reduce_sum | solution.py:338
  562.3 7.6 fusion.131
  583.4 10.3 %fusion.183 = f32[1536,2,768]{2,0,1:T(8,128)} fusion(bf16[1024,1536,1]{1,0,2:T(8,128)(2,1)S(1)} %bitcast.496, bf16[2,768,1024]{2,1,0:T(8,128)(2,1)} %bitcast.514), kind=kOutput, calls=%fused_computation.295 | convolution fusion | flops 4831838208 | bytes 15728640 | tf_op jit(solution)/shard_map/dot_general | solution.py:48
  593.8 7.7 convolution_bitcast_fusion
  614.4 24.4 %all-reduce.5 = (f32[1024,4]{0,1:T(4,128)S(1)}, f32[1536,4]{0,1:T(4,128)S(1)}) all-reduce(f32[1024,4]{0,1:T(4,128)S(1)} %broadcast_in_dim.151, f32[1536,4]{0,1:T(4,128)S(1)} %broadcast_in_dim.152), channel_id=7, replica_groups=mesh['shard'=2,'ctx'=4,'tensor'=4] {'tensor'}, use_global_device_ids=true, to_apply=%region_28.29.clone | all-reduce | flops 10240 | bytes 81920
  639.6 28.3 %all-reduce.4 = (f32[1536]{0:T(1024)S(1)}, f32[4,768]{1,0:T(4,128)}, f32[768]{0:T(1024)}, f32[4,256]{1,0:T(4,128)}, f32[256]{0:T(256)}, /*index=5*/f32[12]{0:T(128)}, f32[12]{0:T(128)}, f32[12]{0:T(128)}, f32[768]{0:T(1024)}) all-reduce(f32[1536]{0:T(1024)S(1)} %add.360, ...), channel_id=9, replica_groups=mesh['shard'=2,'ctx'=4,'tensor'=4] {'shard','ctx'}, use_global_device_ids=true, to_apply=%region_33.34.clone | all-reduce | flops 7460 | bytes 59680
  669.2 21.3 %reduce-scatter.11.cloned.1.call-done = f32[2,512,384]{2,1,0:T(8,128)} async-done(((f32[2,512,1536]{2,1,0:T(8,128)}), f32[2,512,384]{2,1,0:T(8,128)}) %reduce-scatter.11.cloned.1.call-update) | async-done | bytes 1572880 | tf_op jit(solution)/shard_map/reduce_scatter | solution.py:297
  693.1 110.8 %reduce-scatter.13.cloned.1.call-done = f32[1024,384]{1,0:T(8,128)} async-done(((f32[1024,1536]{1,0:T(8,128)}), f32[1024,384]{1,0:T(8,128)}) %reduce-scatter.13.cloned.1.call-update) | async-done | bytes 1572880 | tf_op jit(solution)/shard_map/reduce_scatter | solution.py:361
  808.0 76.7 %reduce-scatter.15.cloned.1.call-done = f32[192,2,768]{2,0,1:T(8,128)} async-done(((f32[1536,2,768]{2,0,1:T(8,128)}), f32[192,2,768]{2,0,1:T(8,128)}) %reduce-scatter.15.cloned.1.call-update) | async-done | bytes 1179664 | tf_op jit(solution)/shard_map/reduce_scatter | solution.py:380
  887.8 54.5 %reduce-scatter.21.cloned.1.call-done = f32[192,768]{1,0:T(8,128)} async-done(((f32[1536,768]{1,0:T(8,128)}), f32[192,768]{1,0:T(8,128)}) %reduce-scatter.21.cloned.1.call-update) | async-done | bytes 589840
  942.3 42.3 %reduce-scatter.17.cloned.1.call-done = f32[192,256]{1,0:T(8,128)} async-done(((f32[1536,256]{1,0:T(8,128)}), f32[192,256]{1,0:T(8,128)}) %reduce-scatter.17.cloned.1.call-update) | async-done | bytes 196624 | tf_op jit(solution)/shard_map/reduce_scatter | solution.py:381
  (521 shorter events, 348.6 us)
Async XLA Ops:
  7.2 76.4 %all-gather.11.cloned.1.call-start = ((), (), s32[]{:S(2)}) async-start(), calls=%async_computation.6 | async-start | bytes 3932160 | tf_op jit(solution)/shard_map/all_gather | solution.py:222
  7.9 106.9 %all-gather.13.cloned.1.call-start = ((), (), s32[]{:S(2)}) async-start(), calls=%async_computation.7 | async-start | bytes 5308416 | tf_op jit(solution)/shard_map/all_gather | solution.py:228
  8.7 187.6 %all-gather.19.cloned.1.call-start = ((), (), s32[]{:S(2)}) async-start(), calls=%async_computation.15 | async-start | bytes 3932160 | tf_op jit(solution)/shard_map/all_gather | solution.py:21
  27.4 72.0 %copy-start.47 = (f32[1536]{0:T(1024)}, f32[1536]{0:T(1024)S(1)}, u32[]{:S(2)}) copy-start(f32[1536]{0:T(1024)S(1)} %convert_element_type.76) | copy-start | bytes 18436
  52.4 31.1 %copy-start.43 = (bf16[8,192,12]{1,0,2:T(8,128)(2,1)}, bf16[8,192,12]{1,0,2:T(8,128)(2,1)S(1)}, u32[]{:S(2)}) copy-start(bf16[8,192,12]{1,0,2:T(8,128)(2,1)S(1)} %copy.360) | copy-start | bytes 110596
  53.4 77.7 %copy-start.54 = (f32[768]{0:T(1024)}, f32[768]{0:T(1024)S(1)}, u32[]{:S(2)}) copy-start(f32[768]{0:T(1024)S(1)} %get-tuple-element.881) | copy-start | bytes 9220
  53.5 77.7 %copy-start.56 = (f32[768]{0:T(1024)}, f32[768]{0:T(1024)S(1)}, u32[]{:S(2)}) copy-start(f32[768]{0:T(1024)S(1)} %get-tuple-element.882) | copy-start | bytes 9220
  53.5 77.7 %copy-start.58 = (f32[768]{0:T(1024)}, f32[768]{0:T(1024)S(1)}, u32[]{:S(2)}) copy-start(f32[768]{0:T(1024)S(1)} %get-tuple-element.883) | copy-start | bytes 9220
  53.5 77.7 %copy-start.60 = (f32[768]{0:T(1024)}, f32[768]{0:T(1024)S(1)}, u32[]{:S(2)}) copy-start(f32[768]{0:T(1024)S(1)} %get-tuple-element.884) | copy-start | bytes 9220
  54.1 48.6 %copy-start.74 = (f32[12]{0:T(128)}, f32[12]{0:T(128)S(1)}, u32[]{:S(2)}) copy-start(f32[12]{0:T(128)S(1)} %exponential_negate_fusion) | copy-start | bytes 148
  55.0 86.7 %copy-start.68 = (f32[1,256]{1,0:T(1,128)}, f32[1,256]{1,0:T(1,128)S(1)}, u32[]{:S(2)}) copy-start(f32[1,256]{1,0:T(1,128)S(1)} %get-tuple-element.1002) | copy-start | bytes 3076
  55.0 86.7 %copy-start.69 = (f32[1,256]{1,0:T(1,128)}, f32[1,256]{1,0:T(1,128)S(1)}, u32[]{:S(2)}) copy-start(f32[1,256]{1,0:T(1,128)S(1)} %get-tuple-element.1003) | copy-start | bytes 3076
  55.0 86.7 %copy-start.70 = (f32[1,256]{1,0:T(1,128)}, f32[1,256]{1,0:T(1,128)S(1)}, u32[]{:S(2)}) copy-start(f32[1,256]{1,0:T(1,128)S(1)} %get-tuple-element.1004) | copy-start | bytes 3076
  55.0 86.7 %copy-start.71 = (f32[1,256]{1,0:T(1,128)}, f32[1,256]{1,0:T(1,128)S(1)}, u32[]{:S(2)}) copy-start(f32[1,256]{1,0:T(1,128)S(1)} %get-tuple-element.1005) | copy-start | bytes 3076
  102.8 27.1 %copy-start.30 = (bf16[1024,256]{1,0:T(8,128)(2,1)}, bf16[1024,256]{1,0:T(8,128)(2,1)S(1)}, u32[]{:S(2)}) copy-start(bf16[1024,256]{1,0:T(8,128)(2,1)S(1)} %fusion.137) | copy-start | bytes 1572868
  126.3 4.8 collective-permute-start
  146.9 18.4 %copy-start.19 = (f32[2,512,768]{1,2,0:T(8,128)S(1)}, f32[2,512,768]{1,2,0:T(8,128)}, u32[]{:S(2)}) copy-start(f32[2,512,768]{1,2,0:T(8,128)} %copy.367) | copy-start | bytes 9437188
  150.8 154.6 %all-gather.15.cloned.1.call-start = ((), (), s32[]{:S(2)}) async-start(), calls=%async_computation.8 | async-start | bytes 2654208 | tf_op jit(solution)/shard_map/all_gather | solution.py:231
  151.3 154.0 %all-gather.17.cloned.1.call-start = ((), (), s32[]{:S(2)}) async-start(), calls=%async_computation.10 | async-start | bytes 3932160 | tf_op jit(solution)/shard_map/all_gather | solution.py:223
  151.9 238.6 %all-gather.21.cloned.1.call-start = ((), (), s32[]{:S(2)}) async-start(), calls=%async_computation.16 | async-start | bytes 3932160 | tf_op jit(solution)/shard_map/all_gather | solution.py:21
  287.4 18.0 %copy-start.49 = (f32[768]{0:T(1024)S(1)}, f32[768]{0:T(1024)}, u32[]{:S(2)}) copy-start(f32[768]{0:T(1024)} %param.37) | copy-start | bytes 9220
  347.5 194.1 %all-reduce.8.cloned.1.call-start = ((), (), s32[]{:S(2)}) async-start(), calls=%async_computation.11 | async-start | bytes 2097152 | tf_op jit(solution)/shard_map/psum | solution.py:328
  485.8 127.0 %reduce-scatter.19.cloned.1.call-start = ((), (), s32[]{:S(2)}) async-start(), calls=%async_computation.17 | async-start | bytes 884736
  499.0 191.5 %reduce-scatter.11.cloned.1.call-start = ((), (), s32[]{:S(2)}) async-start(), calls=%async_computation.9 | async-start | bytes 7864320 | tf_op jit(solution)/shard_map/reduce_scatter | solution.py:297
  507.0 296.9 %reduce-scatter.13.cloned.1.call-start = ((), (), s32[]{:S(2)}) async-start(), calls=%async_computation.12 | async-start | bytes 7864320 | tf_op jit(solution)/shard_map/reduce_scatter | solution.py:361
  547.4 6.0 collective-permute-start.1
  574.9 309.7 %reduce-scatter.15.cloned.1.call-start = ((), (), s32[]{:S(2)}) async-start(), calls=%async_computation.13 | async-start | bytes 10616832 | tf_op jit(solution)/shard_map/reduce_scatter | solution.py:380
  593.8 348.6 %reduce-scatter.21.cloned.1.call-start = ((), (), s32[]{:S(2)}) async-start(), calls=%async_computation.18 | async-start | bytes 5308416
  607.8 31.8 %copy-start.77 = (f32[256]{0:T(256)S(1)}, f32[256]{0:T(256)}, u32[]{:S(2)}) copy-start(f32[256]{0:T(256)} %get-tuple-element.876) | copy-start | bytes 3076
  607.8 31.8 %copy-start.82 = (f32[768]{0:T(1024)S(1)}, f32[768]{0:T(1024)}, u32[]{:S(2)}) copy-start(f32[768]{0:T(1024)} %get-tuple-element.864) | copy-start | bytes 9220
  607.8 31.8 %copy-start.83 = (f32[12]{0:T(128)S(1)}, f32[12]{0:T(128)}, u32[]{:S(2)}) copy-start(f32[12]{0:T(128)} %get-tuple-element.969) | copy-start | bytes 148
  607.8 376.8 %reduce-scatter.17.cloned.1.call-start = ((), (), s32[]{:S(2)}) async-start(), calls=%async_computation.14 | async-start | bytes 1769472 | tf_op jit(solution)/shard_map/reduce_scatter | solution.py:381
  (89 other events, 398.0 us)
Sparse Core Ops, SparseCore 0:
  9.6 65.9 all-gather.10
  77.4 37.3 all-gather.12
  150.9 45.3 all-gather.18
  198.0 28.8 all-gather.14
  228.3 63.4 all-gather.16
  347.6 42.8 all-gather.20
  485.9 51.8 all-reduce.7
  541.5 34.2 reduce-scatter.18
  578.1 112.3 reduce-scatter.10
  692.6 111.2 reduce-scatter.12
  807.4 77.1 reduce-scatter.14
  888.5 53.7 reduce-scatter.20
  946.2 38.3 reduce-scatter.16
where the time goes:
time: 1000 us; the launch traced here: 992 us
  waiting for transfers between devices  380 us (38%)
  local copies, waits for them, and re-layouts  169 us (17%)
  matrix products  155 us (16%)
  blocking collectives  151 us (15%)
  other arithmetic  114 us (11%)
  between operations  16.8 us (2%)
    reduce_scatter x1, waiting for transfers between devices, body(): lax.psum_scatter(local_part, 'tensor', scatter_dimension=1, tiled=True)  111 us
    reduce_scatter x1, waiting for transfers between devices, body(): lax.psum_scatter(gate_value_grad, ('shard', 'ctx'), scatter_dimension=0,...  76.7 us
    unnamed x3, blocking collectives  68.6 us
    all_gather x2, waiting for transfers between devices, entering(): pieces = jax.tree.map(lambda part: lax.all_gather(part, axis), value)  59.4 us
    unnamed x15, waiting for transfers between devices  57.1 us
    reduce_scatter x1, waiting for transfers between devices, body(): lax.psum_scatter(matrix_grad, ('shard', 'ctx'), scatter_dimension=0, tile...  42.3 us
    unnamed x160, local copies, waits for them, and re-layouts  33.1 us
    all_gather x1, blocking collectives, body(): lax.all_gather(matrix_weight, ('shard', 'ctx'), axis=0, tiled=True)  28.6 us
  transfers between devices with their start and end apart: 15, of which 9 were waited for; matrix products, arithmetic and copies ran while one was open for 27% of the time, Pallas kernels for 0%

commit v1 on v0

v1 whole, which is shorter than its diff:
```python
import functools

import jax
import jax.numpy as jnp
from jax import lax
from jax.experimental import pallas as pl
from jax.experimental.pallas import tpu as pltpu
from jax.sharding import PartitionSpec as P

EPSILON = 1e-05
HALO = 16
CHUNK = 128
LANES = 128
HIGHEST = lax.Precision.HIGHEST
MESH = pl.DeviceIdType.MESH
F32 = jnp.float32
BF16 = jnp.bfloat16
VMEM_ALL = 64000 * 1024
FINE_A = True
FINE_B = True
FINE_C = True
FINE_S = True


def dot_nn(left, right, precision=None):
    return lax.dot_general(
        left, right, (((1,), (0,)), ((), ())), precision=precision, preferred_element_type=F32
    )


def dot_nt(left, right, precision=None):
    return lax.dot_general(
        left, right, (((1,), (1,)), ((), ())), precision=precision, preferred_element_type=F32
    )


def dot_tokens(left, right):
    axes = tuple(range(left.ndim - 1))
    return lax.dot_general(left, right, ((axes, axes), ((), ())), preferred_element_type=F32)


def split(value):
    high = value.astype(BF16)
    return high, (value - high.astype(F32)).astype(BF16)


def fine(dot, left, right):
    (a, b), (c, d) = split(left), split(right)
    return dot(a, c) + (dot(a, d) + dot(b, c))


def vmem_spec():
    return pl.BlockSpec(memory_space=pltpu.VMEM)


def any_spec():
    return pl.BlockSpec(memory_space=pl.ANY)


def sizes():
    return lax.axis_size("shard"), lax.axis_size("ctx"), lax.axis_size("tensor")


def places():
    return lax.axis_index("shard"), lax.axis_index("ctx"), lax.axis_index("tensor")


def remote(src, dst, send_sem, recv_sem, **device):
    return pltpu.make_async_remote_copy(
        src_ref=src,
        dst_ref=dst,
        send_sem=send_sem,
        recv_sem=recv_sem,
        device_id=device,
        device_id_type=MESH,
    )


def greet(peers, count):
    barrier = pltpu.get_barrier_semaphore()
    for condition, device in peers:
        if condition is None:
            pl.semaphore_signal(barrier, inc=1, device_id=device, device_id_type=MESH)
        else:

            @pl.when(condition)
            def _():
                pl.semaphore_signal(barrier, inc=1, device_id=device, device_id_type=MESH)

    pl.semaphore_wait(barrier, count)


def gather_kernel(
    dims, x_ref, gv_ref, ow_ref, sw_ref, X, GV, OW, SW, hv, lsem, hs, hr, zs, zr, cs, cr, ss, sr
):
    ns, nc, nz = dims
    s, c, z = places()
    seqs, length, quarter = x_ref.shape
    half = length // 2
    parts = [(q, h * half) for q in range(seqs) for h in range(2)]
    count = len(parts)

    peers = [(z > 0, {"tensor": z - 1}), (z < nz - 1, {"tensor": z + 1})]
    peers += [(None, {"ctx": lax.rem(c + k, nc)}) for k in range(1, nc)]
    peers += [(None, {"shard": lax.rem(s + j, ns)}) for j in range(1, ns)]
    greet(
        peers,
        jnp.where(z > 0, 1, 0) + jnp.where(z < nz - 1, 1, 0) + (nc - 1) + (ns - 1),
    )

    def columns(owner):
        return pl.ds(pl.multiple_of(owner * quarter, quarter), quarter)

    def region(i, owner):
        if i == count:
            return X.at[:, pl.ds(0, HALO), columns(owner)]
        q, r0 = parts[i]
        return X.at[q, pl.ds(HALO + r0, half), columns(owner)]

    def own(i):
        if i == count:
            return hv
        q, r0 = parts[i]
        return x_ref.at[q, pl.ds(r0, half), :]

    def up(d, i):
        src = own(i) if d == 0 else region(i, z - d)
        return remote(src, region(i, z - d), zs.at[0, d, i], zr.at[0, d, i], tensor=z + 1)

    def down(d, i):
        src = own(i) if d == 0 else region(i, z + d)
        return remote(src, region(i, z + d), zs.at[1, d, i], zr.at[1, d, i], tensor=z - 1)

    def got_up(d, i):
        here = region(i, z - d)
        return remote(here, here, zs.at[0, d - 1, i], zr.at[0, d - 1, i], tensor=z - 1)

    def got_down(d, i):
        here = region(i, z + d)
        return remote(here, here, zs.at[1, d - 1, i], zr.at[1, d - 1, i], tensor=z + 1)

    halo_send = remote(
        x_ref.at[:, pl.ds(length - HALO, HALO), :], hv, hs, hr, ctx=lax.rem(c + 1, nc)
    )

    @pl.when(c < nc - 1)
    def _():
        halo_send.start()

    for i in range(count):

        @pl.when(z < nz - 1)
        def _():
            up(0, i).start()

        @pl.when(z > 0)
        def _():
            down(0, i).start()

    arrays = [(gv_ref, GV), (ow_ref, OW), (sw_ref, SW)]

    def rows(array, shard, ctx):
        block = array[0].shape[0]
        return array[1].at[pl.ds(pl.multiple_of((shard * nc + ctx) * block, block), block), :]

    def to_ctx(k, a):
        array = arrays[a]
        return remote(
            array[0], rows(array, s, c), cs.at[k - 1, a], cr.at[k - 1, a], ctx=lax.rem(c + k, nc)
        )

    def from_ctx(k, a):
        here = rows(arrays[a], s, lax.rem(c + nc - k, nc))
        return remote(
            here, here, cs.at[k - 1, a], cr.at[k - 1, a], ctx=lax.rem(c + nc - k, nc)
        )

    def to_shard(k, j, a):
        array = arrays[a]
        there = rows(array, s, lax.rem(c + nc - k, nc))
        src = array[0] if k == 0 else there
        return remote(
            src, there, ss.at[k, j - 1, a], sr.at[k, j - 1, a], shard=lax.rem(s + j, ns)
        )

    def from_shard(k, j, a):
        owner = lax.rem(s + ns - j, ns)
        here = rows(arrays[a], owner, lax.rem(c + nc - k, nc))
        return remote(here, here, ss.at[k, j - 1, a], sr.at[k, j - 1, a], shard=owner)

    for a in range(3):
        for k in range(1, nc):
            to_ctx(k, a).start()
        for j in range(1, ns):
            to_shard(0, j, a).start()

    local = [pltpu.make_async_copy(x_ref, X.at[:, pl.ds(HALO, length), columns(z)], lsem.at[0])]
    local += [
        pltpu.make_async_copy(array[0], rows(array, s, c), lsem.at[1 + a])
        for a, array in enumerate(arrays)
    ]
    for copy in local:
        copy.start()

    @pl.when(c == 0)
    def _():
        hv[...] = jnp.zeros_like(hv)

    @pl.when(c > 0)
    def _():
        remote(hv, hv, hs, hr, ctx=lax.rem(c + nc - 1, nc)).wait_recv()

    @pl.when(z < nz - 1)
    def _():
        up(0, count).start()

    @pl.when(z > 0)
    def _():
        down(0, count).start()

    halo_copy = pltpu.make_async_copy(hv, X.at[:, pl.ds(0, HALO), columns(z)], lsem.at[4])
    halo_copy.start()

    for d in range(1, nz):
        for i in range(count + 1):

            @pl.when(z - d >= 0)
            def _():
                got_up(d, i).wait_recv()
                if d < nz - 1:

                    @pl.when(z < nz - 1)
                    def _():
                        up(d, i).start()

            @pl.when(z + d < nz)
            def _():
                got_down(d, i).wait_recv()
                if d < nz - 1:

                    @pl.when(z > 0)
                    def _():
                        down(d, i).start()

        if d == max(1, nz - 2):
            for a in range(3):
                for k in range(1, nc):
                    from_ctx(k, a).wait_recv()
                    for j in range(1, ns):
                        to_shard(k, j, a).start()

    for a in range(3):
        for k in range(nc):
            for j in range(1, ns):
                from_shard(k, j, a).wait_recv()
    for copy in local:
        copy.wait()
    halo_copy.wait()

    @pl.when(c < nc - 1)
    def _():
        halo_send.wait_send()

    for d in range(nz - 1):
        for i in range(count + 1):

            @pl.when((z - d >= 0) & (z < nz - 1))
            def _():
                up(d, i).wait_send()

            @pl.when((z + d < nz) & (z > 0))
            def _():
                down(d, i).wait_send()

    for a in range(3):
        for k in range(1, nc):
            to_ctx(k, a).wait_send()
        for k in range(nc):
            for j in range(1, ns):
                to_shard(k, j, a).wait_send()


def gather(x, gv, ow, sw):
    ns, nc, nz = dims = sizes()
    seqs, length, quarter = x.shape
    shapes = [(seqs, length + HALO, quarter * nz)] + [(w.shape[0] * ns * nc, w.shape[1]) for w in (gv, ow, sw)]
    parts = 2 * seqs + 1
    dma = pltpu.SemaphoreType.DMA
    return pl.pallas_call(
        functools.partial(gather_kernel, dims),
        out_shape=[jax.ShapeDtypeStruct(shape, BF16) for shape in shapes],
        in_specs=[vmem_spec()] * 4,
        out_specs=[any_spec()] * 4,
        scratch_shapes=[
            pltpu.VMEM((seqs, HALO, quarter), BF16),
            dma((5,)),
            dma,
            dma,
            dma((2, nz - 1, parts)),
            dma((2, nz - 1, parts)),
            dma((nc - 1, 3)),
            dma((nc - 1, 3)),
            dma((nc, ns - 1, 3)),
            dma((nc, ns - 1, 3)),
        ],
        compiler_params=pltpu.CompilerParams(
            collective_id=0, has_side_effects=True, vmem_limit_bytes=VMEM_ALL
        ),
        name="gather",
    )(x, gv, ow, sw)


def project_kernel(x_ref, gain_ref, gv_ref, sw_ref, normed_ref, out_ref, small_ref, scale_ref):
    u = x_ref[0].astype(F32)
    scale = lax.rsqrt(jnp.mean(u * u, axis=1, keepdims=True) + EPSILON)
    normed = (u * scale * gain_ref[...]).astype(BF16)
    normed_ref[0] = normed
    scale_ref[0] = jnp.broadcast_to(scale, scale_ref.shape[1:])
    out_ref[0] = dot_nn(normed, gv_ref[...]).astype(BF16)
    small_ref[0] = dot_nn(normed, sw_ref[...])


def project(X, gain, GV, SW):
    seqs, rows, width = X.shape
    block = rows // 3
    full = lambda array: pl.BlockSpec(array.shape, lambda q, r: (0, 0))
    tile = lambda cols: pl.BlockSpec((1, block, cols), lambda q, r: (q, r, 0))
    return pl.pallas_call(
        project_kernel,
        grid=(seqs, 3),
        in_specs=[tile(width), full(gain), full(GV), full(SW)],
        out_specs=[tile(width), tile(GV.shape[1]), tile(SW.shape[1]), tile(LANES)],
        out_shape=[
            jax.ShapeDtypeStruct((seqs, rows, width), BF16),
            jax.ShapeDtypeStruct((seqs, rows, GV.shape[1]), BF16),
            jax.ShapeDtypeStruct((seqs, rows, SW.shape[1]), F32),
            jax.ShapeDtypeStruct((seqs, rows, LANES), F32),
        ],
        compiler_params=pltpu.CompilerParams(vmem_limit_bytes=VMEM_ALL),
        name="project",
    )(X, gain, GV, SW)


def sigmoid(value):
    return 1.0 / (1.0 + jnp.exp(-value))


def iota(axis, shape=(CHUNK, LANES)):
    return lax.broadcasted_iota(jnp.int32, shape, axis)


def causal_conv(padded, taps, bias):
    width = taps.shape[0]
    total = bias + taps[width - 1 : width] * padded[HALO:]
    for offset in range(width - 1):
        shifted = pltpu.roll(padded, width - 1 - offset, 0)
        total = total + taps[offset : offset + 1] * shifted[HALO:]
    return total


def conv_back(padded, taps, rows):
    width = taps.shape[0]
    total = taps[width - 1 : width] * padded[:rows]
    for offset in range(width - 1):
        ahead = width - 1 - offset
        shifted = pltpu.roll(padded, padded.shape[0] - ahead, 0)
        total = total + taps[offset : offset + 1] * shifted[:rows]
    return total


def pair(columns, p):
    rows = columns.shape[0]
    first = iota(1, (rows, LANES)) < LANES // 2
    left = jnp.broadcast_to(columns[:, 2 * p : 2 * p + 1], (rows, LANES))
    right = jnp.broadcast_to(columns[:, 2 * p + 1 : 2 * p + 2], (rows, LANES))
    return jnp.where(first, left, right)


def stacked(value):
    first = iota(1, value.shape) < LANES // 2
    zero = jnp.zeros_like(value)
    both = [jnp.where(first, value, zero), jnp.where(first, zero, value)]
    return jnp.concatenate(both, axis=0).astype(BF16)


def head_sums(p):
    rows, cols = iota(0, (LANES, LANES)), iota(1, (LANES, LANES))
    return jnp.where(cols == 2 * p + jnp.where(rows < LANES // 2, 0, 1), 1.0, 0.0)


def softplus(value):
    return jnp.maximum(value, 0.0) + jnp.log1p(jnp.exp(-jnp.abs(value)))


def join_states(own_ref, decay_ref, mine, backward, q):
    count = own_ref.shape[0]
    total = jnp.zeros(own_ref.shape[2:], F32)
    for step in range(count):
        i = count - 1 - step if backward else step
        longer = decay_ref[i, q, 0:1, :] * total + own_ref[i, q].astype(F32)
        total = jnp.where((mine < i) if backward else (i < mine), longer, total)
    return total


def forward_kernel(
    heads,
    gv_ref,
    small_ref,
    vk_ref,
    vb_ref,
    mk_ref,
    mb_ref,
    sb_ref,
    rate_ref,
    v_ref,
    slope_ref,
    y_ref,
    starts_ref,
    own_ref,
    step_ref,
    cum_ref,
    carry_ref,
    mat_ref,
    mslope_ref,
    end_ref,
    state,
    carry,
):
    k = pl.program_id(1)

    @pl.when(k == 0)
    def _():
        state[...] = jnp.zeros_like(state)
        carry[...] = jnp.zeros_like(carry)

    rows = pl.ds(pl.multiple_of(k * CHUNK, CHUNK), CHUNK + HALO)
    small = small_ref[0, rows, :]
    mwidth = mk_ref.shape[1]
    matrix_in = small[:, :mwidth].astype(BF16).astype(F32)
    mconv = causal_conv(matrix_in, mk_ref[...], mb_ref[...])
    msig = sigmoid(mconv)
    mat = mconv * msig
    mat_ref[0] = mat
    mslope_ref[0] = msig * (1.0 + mconv * (1.0 - msig))
    b_mat, c_mat = mat[:, : mwidth // 2], mat[:, mwidth // 2 :]
    b_low, c_low = b_mat.astype(BF16), c_mat.astype(BF16)
    bt_low = b_mat.T.astype(BF16)
    gram = dot_nt(c_low, b_low)

    lane = iota(1)
    raw = small[HALO:, mwidth:] + sb_ref[...]
    step = jnp.where(lane < heads, softplus(raw), 0.0)
    tri = jnp.where(iota(0) >= lane, 1.0, 0.0)
    cum = dot_nn(tri, step * rate_ref[...], HIGHEST)
    cum_t = cum.T
    step_ref[0] = step
    cum_ref[0] = cum
    carry_ref[0, 0] = carry[...]
    last = cum[CHUNK - 1 : CHUNK, :]
    carry[...] = carry[...] + last
    from_start = jnp.exp(cum)
    to_end = jnp.exp(last - cum)
    whole = jnp.exp(last)
    causal = iota(0) >= lane

    for p in range(heads // 2):
        cols = slice(p * LANES, (p + 1) * LANES)
        signal = gv_ref[0, rows, cols].astype(F32)
        conv = causal_conv(signal, vk_ref[:, cols], vb_ref[:, cols])
        sig = sigmoid(conv)
        v = conv * sig
        v_ref[0, :, cols] = v
        slope_ref[0, :, cols] = sig * (1.0 + conv * (1.0 - sig))
        scaled = v * pair(step, p)
        weights = []
        for h in (2 * p, 2 * p + 1):
            spread = cum[:, h : h + 1] - cum_t[h : h + 1, :]
            weights.append(jnp.where(causal, jnp.exp(spread) * gram, 0.0))
        weights = jnp.concatenate(weights, axis=1).astype(BF16)
        old = state[:, cols]
        starts_ref[0, 0, :, cols] = old
        y = dot_nn(weights, stacked(scaled))
        y = y + pair(from_start, p) * dot_nn(c_low, old.astype(BF16))
        y_ref[0, :, cols] = y
        new = dot_nn(bt_low, (scaled * pair(to_end, p)).astype(BF16))
        state[:, cols] = pair(whole, p) * old + new

    @pl.when(k == pl.num_programs(1) - 1)
    def _():
        own_ref[0] = state[...].astype(own_ref.dtype)
        end = jnp.exp(carry[...])
        for p in range(heads // 2):
            end_ref[0, :, p * LANES : (p + 1) * LANES] = pair(end, p)


def forward(gate_value, small, vk, vb, mk, mb, sb, rate, heads):
    seqs, rows, width = gate_value.shape
    inner = width // 2
    length = rows - HALO
    chunks = length // CHUNK
    state_width = mk.shape[1] // 2
    full = lambda array: pl.BlockSpec(array.shape, lambda q, k: (0, 0))
    tile = lambda cols: pl.BlockSpec((1, CHUNK, cols), lambda q, k: (q, k, 0))
    out = [
        ((seqs, length, inner), F32, tile(inner)),
        ((seqs, length, inner), F32, tile(inner)),
        ((seqs, length, inner), F32, tile(inner)),
        (
            (seqs, chunks, state_width, inner),
            F32,
            pl.BlockSpec((1, 1, state_width, inner), lambda q, k: (q, k, 0, 0)),
        ),
        (
            (seqs, state_width, inner),
            F32 if FINE_S else BF16,
            pl.BlockSpec((1, state_width, inner), lambda q, k: (q, 0, 0)),
        ),
        ((seqs, length, LANES), F32, tile(LANES)),
        ((seqs, length, LANES), F32, tile(LANES)),
        ((seqs, chunks, 8, LANES), F32, pl.BlockSpec((1, 1, 8, LANES), lambda q, k: (q, k, 0, 0))),
        ((seqs, length, 2 * state_width), F32, tile(2 * state_width)),
        ((seqs, length, 2 * state_width), F32, tile(2 * state_width)),
        ((seqs, 8, inner), F32, pl.BlockSpec((1, 8, inner), lambda q, k: (q, 0, 0))),
    ]
    return pl.pallas_call(
        functools.partial(forward_kernel, heads),
        grid=(seqs, chunks),
        in_specs=[
            pl.BlockSpec((1, rows, inner), lambda q, k: (q, 0, 1)),
            pl.BlockSpec((1, rows, small.shape[2]), lambda q, k: (q, 0, 0)),
        ]
        + [full(array) for array in (vk, vb, mk, mb, sb, rate)],
        out_specs=[spec for _, _, spec in out],
        out_shape=[jax.ShapeDtypeStruct(shape, dtype) for shape, dtype, _ in out],
        scratch_shapes=[pltpu.VMEM((state_width, inner), F32), pltpu.VMEM((8, LANES), F32)],
        compiler_params=pltpu.CompilerParams(vmem_limit_bytes=VMEM_ALL),
        name="forward",
    )(gate_value, small, vk, vb, mk, mb, sb, rate)


def exchange_kernel(dims, backward, own_ref, end_ref, all_ref, ends_ref, lsem, ss, sr, es, er):
    ns, nc, nz = dims
    s, c, z = places()
    greet([(None, {"ctx": lax.rem(c + k, nc)}) for k in range(1, nc)], nc - 1)

    def state(k):
        there = c - k if backward else c + k
        return remote(
            own_ref, all_ref.at[c], ss.at[k - 1], sr.at[k - 1], ctx=lax.rem(there + nc, nc)
        )

    def arrived(k):
        owner = lax.rem((c + k if backward else c - k) + nc, nc)
        return remote(own_ref, all_ref.at[owner], ss.at[k - 1], sr.at[k - 1], ctx=owner)

    def ends(k):
        return remote(
            end_ref, ends_ref.at[c], es.at[k - 1], er.at[k - 1], ctx=lax.rem(c + k, nc)
        )

    def ends_arrived(k):
        owner = lax.rem(c + nc - k, nc)
        return remote(end_ref, ends_ref.at[owner], es.at[k - 1], er.at[k - 1], ctx=owner)

    def sends(k):
        return (c - k >= 0) if backward else (c + k < nc)

    def receives(k):
        return (c + k < nc) if backward else (c - k >= 0)

    for k in range(1, nc):

        @pl.when(sends(k))
        def _():
            state(k).start()

        if not backward:
            ends(k).start()
    copies = [pltpu.make_async_copy(own_ref, all_ref.at[c], lsem.at[0])]
    if not backward:
        copies.append(pltpu.make_async_copy(end_ref, ends_ref.at[c], lsem.at[1]))
    for copy in copies:
        copy.start()
    for k in range(1, nc):

        @pl.when(receives(k))
        def _():
            arrived(k).wait_recv()

        if not backward:
            ends_arrived(k).wait_recv()
    for copy in copies:
        copy.wait()
    for k in range(1, nc):

        @pl.when(sends(k))
        def _():
            state(k).wait_send()

        if not backward:
            ends(k).wait_send()


def exchange(own, end, backward):
    ns, nc, nz = dims = sizes()
    dma = pltpu.SemaphoreType.DMA
    return pl.pallas_call(
        functools.partial(exchange_kernel, dims, backward),
        out_shape=[
            jax.ShapeDtypeStruct((nc,) + own.shape, own.dtype),
            jax.ShapeDtypeStruct((nc,) + end.shape, end.dtype),
        ],
        in_specs=[vmem_spec()] * 2,
        out_specs=[any_spec()] * 2,
        scratch_shapes=[dma((2,))] + [dma((nc - 1,))] * 4,
        compiler_params=pltpu.CompilerParams(
            collective_id=2 if backward else 1, has_side_effects=True
        ),
        name="adjoints" if backward else "states",
    )(own, end)


def gate_kernel(
    heads,
    y_ref,
    v_ref,
    gv_ref,
    cot_ref,
    ow_ref,
    cum_ref,
    carry_ref,
    mat_ref,
    all_ref,
    ends_ref,
    ig_ref,
    skip_ref,
    ssd_ref,
    grad_inner_ref,
    sums_ref,
    start_ref,
):
    q, k = pl.program_id(0), pl.program_id(1)

    @pl.when(k == 0)
    def _():
        start_ref[0] = join_states(all_ref, ends_ref, lax.axis_index("ctx"), False, 0)

    rows = pl.ds(pl.multiple_of(HALO + k * CHUNK, HALO), CHUNK)
    half = mat_ref.shape[2] // 2
    c_low = mat_ref[0, :, half:].astype(BF16)
    from_start = jnp.exp(cum_ref[0] + carry_ref[0, 0, 0:1, :])
    grad_inner = dot_nn(cot_ref[0], ow_ref[...])
    grad_inner_ref[0] = grad_inner
    squares = jnp.zeros((CHUNK, LANES), F32)
    dots = jnp.zeros((CHUNK, LANES), F32)
    for p in range(heads // 2):
        cols = slice(p * LANES, (p + 1) * LANES)
        carried = dot_nn(c_low, start_ref[0, :, cols].astype(BF16))
        ssd = y_ref[0, :, cols] + pair(from_start, p) * carried
        ssd_ref[0, :, cols] = ssd
        gate = gv_ref[0, rows, cols].astype(F32)
        mixed = ssd + skip_ref[:, cols] * v_ref[0, :, cols]
        gated = mixed * (gate * sigmoid(gate))
        squares = squares + gated * gated
        dots = dots + grad_inner[:, cols] * ig_ref[:, cols] * gated
    ones = jnp.ones((8, LANES), F32)
    first = iota(0, (8, CHUNK)) == 0
    sums_ref[0] = jnp.where(first, dot_nt(ones, squares, HIGHEST), dot_nt(ones, dots, HIGHEST))


def gate_step(y, v, gate_value, cot, OW, cum, carry, mat, all_states, ends, ig, skip, heads):
    seqs, length, inner = y.shape
    rows = gate_value.shape[1]
    chunks = length // CHUNK
    count, _, state_width, _ = all_states.shape
    width = cot.shape[2]
    full = lambda array: pl.BlockSpec(array.shape, lambda q, k: (0, 0))
    tile = lambda cols: pl.BlockSpec((1, CHUNK, cols), lambda q, k: (q, k, 0))
    return pl.pallas_call(
        functools.partial(gate_kernel, heads),
        grid=(seqs, chunks),
        in_specs=[
            tile(inner),
            tile(inner),
            pl.BlockSpec((1, rows, inner), lambda q, k: (q, 0, 0)),
            tile(width),
            full(OW),
            tile(LANES),
            pl.BlockSpec((1, 1, 8, LANES), lambda q, k: (q, k, 0, 0)),
            tile(2 * state_width),
            pl.BlockSpec((count, 1, state_width, inner), lambda q, k: (0, q, 0, 0)),
            pl.BlockSpec((count, 1, 8, inner), lambda q, k: (0, q, 0, 0)),
            full(ig),
            full(skip),
        ],
        out_specs=[
            tile(inner),
            tile(inner),
            pl.BlockSpec((1, 8, CHUNK), lambda q, k: (q, 0, k)),
            pl.BlockSpec((1, state_width, inner), lambda q, k: (q, 0, 0)),
        ],
        out_shape=[
            jax.ShapeDtypeStruct((seqs, length, inner), F32),
            jax.ShapeDtypeStruct((seqs, length, inner), F32),
            jax.ShapeDtypeStruct((seqs, 8, length), F32),
            jax.ShapeDtypeStruct((seqs, state_width, inner), F32),
        ],
        compiler_params=pltpu.CompilerParams(vmem_limit_bytes=VMEM_ALL),
        name="gates",
    )(y, v, gate_value, cot, OW, cum, carry, mat, all_states, ends, ig, skip)


def token_sum_kernel(dims, own_ref, total_ref, slots, ss, sr):
    ns, nc, nz = dims
    s, c, z = places()
    greet([(None, {"tensor": lax.rem(z + k, nz)}) for k in range(1, nz)], nz - 1)

    def send(k):
        return remote(
            own_ref, slots.at[k - 1], ss.at[k - 1], sr.at[k - 1], tensor=lax.rem(z + k, nz)
        )

    for k in range(1, nz):
        send(k).start()
    total = own_ref[...]
    for k in range(1, nz):
        send(k).wait_recv()
        total = total + slots[k - 1]
    total_ref[...] = total
    for k in range(1, nz):
        send(k).wait_send()


def token_sum(own):
    ns, nc, nz = dims = sizes()
    dma = pltpu.SemaphoreType.DMA
    return pl.pallas_call(
        functools.partial(token_sum_kernel, dims),
        out_shape=jax.ShapeDtypeStruct(own.shape, F32),
        in_specs=[vmem_spec()],
        out_specs=vmem_spec(),
        scratch_shapes=[pltpu.VMEM((nz - 1,) + own.shape, F32)] + [dma((nz - 1,))] * 2,
        compiler_params=pltpu.CompilerParams(collective_id=3, has_side_effects=True),
        name="token_sum",
    )(own)


def mixed_kernel(
    heads,
    inner_total,
    ssd_ref,
    v_ref,
    gv_ref,
    grad_inner_ref,
    sums_ref,
    ow_ref,
    cum_ref,
    carry_ref,
    mat_ref,
    ig_ref,
    skip_ref,
    gm_ref,
    gate_ref,
    inner_ref,
    part_ref,
    adjoint_ref,
    vec_ref,
    total,
):
    q, k = pl.program_id(0), pl.program_id(1)

    @pl.when(k == 0)
    def _():
        total[...] = jnp.zeros_like(total)
        gate_ref[0, 0:HALO, :] = jnp.zeros((HALO, gate_ref.shape[2]), BF16)

    @pl.when((k == 0) & (q == 0))
    def _():
        vec_ref[...] = jnp.zeros_like(vec_ref)

    rows = pl.ds(pl.multiple_of(HALO + k * CHUNK, HALO), CHUNK)
    half = mat_ref.shape[2] // 2
    ct_low = mat_ref[0, :, half:].T.astype(BF16)
    from_start = jnp.exp(cum_ref[0] + carry_ref[0, 0, 0:1, :])
    sums = sums_ref[0].T
    scale = lax.rsqrt(sums[:, 0:1] / inner_total + EPSILON)
    row_dot = sums[:, 1:2] / inner_total
    scale = jnp.broadcast_to(scale, (CHUNK, LANES))
    back = scale * scale * scale * jnp.broadcast_to(row_dot, (CHUNK, LANES))
    for p in range(heads // 2):
        cols = slice(p * LANES, (p + 1) * LANES)
        v = v_ref[0, :, cols]
        mixed = ssd_ref[0, :, cols] + skip_ref[:, cols] * v
        gate = gv_ref[0, rows, cols].astype(F32)
        sig = sigmoid(gate)
        act = gate * sig
        gated = mixed * act
        grad_inner = grad_inner_ref[0, :, cols]
        normal = gated * scale
        inner_ref[0, :, cols] = (normal * ig_ref[:, cols]).astype(BF16)
        grad_gated = scale * (grad_inner * ig_ref[:, cols]) - gated * back
        grad_mixed = grad_gated * act
        gm_ref[0, :, cols] = grad_mixed
        slope = sig * (1.0 + gate * (1.0 - sig))
        gate_ref[0, rows, cols] = (grad_gated * mixed * slope).astype(BF16)
        vec_ref[0:1, cols] += jnp.sum(grad_inner * normal, axis=0, keepdims=True)
        vec_ref[1:2, cols] += jnp.sum(grad_mixed * v, axis=0, keepdims=True)
        total[:, cols] += dot_nn(ct_low, (grad_mixed * pair(from_start, p)).astype(BF16))
    quarter = part_ref.shape[3]
    for j in range(part_ref.shape[0]):
        rows_of = slice(j * quarter, (j + 1) * quarter)
        part_ref[j, 0] = dot_nt(inner_ref[0], ow_ref[rows_of, :]).astype(BF16)

    @pl.when(k == pl.num_programs(1) - 1)
    def _():
        adjoint_ref[0] = total[...].astype(adjoint_ref.dtype)


def mixed_step(
    ssd, v, gate_value, grad_inner, sums, OW, cum, carry, mat, ig, skip, heads, inner_total, nz
):
    seqs, length, inner = ssd.shape
    rows = gate_value.shape[1]
    chunks = length // CHUNK
    state_width = mat.shape[2] // 2
    width = OW.shape[0]
    full = lambda array: pl.BlockSpec(array.shape, lambda q, k: (0, 0))
    tile = lambda cols: pl.BlockSpec((1, CHUNK, cols), lambda q, k: (q, k, 0))
    return pl.pallas_call(
        functools.partial(mixed_kernel, heads, inner_total),
        grid=(seqs, chunks),
        in_specs=[
            tile(inner),
            tile(inner),
            pl.BlockSpec((1, rows, inner), lambda q, k: (q, 0, 0)),
            tile(inner),
            pl.BlockSpec((1, 8, CHUNK), lambda q, k: (q, 0, k)),
            full(OW),
            tile(LANES),
            pl.BlockSpec((1, 1, 8, LANES), lambda q, k: (q, k, 0, 0)),
            tile(2 * state_width),
            full(ig),
            full(skip),
        ],
        out_specs=[
            tile(inner),
            pl.BlockSpec((1, rows, inner), lambda q, k: (q, 0, 0)),
            tile(inner),
            pl.BlockSpec((nz, 1, CHUNK, width // nz), lambda q, k: (0, q, k, 0)),
            pl.BlockSpec((1, state_width, inner), lambda q, k: (q, 0, 0)),
            pl.BlockSpec((8, inner), lambda q, k: (0, 0)),
        ],
        out_shape=[
            jax.ShapeDtypeStruct((seqs, length, inner), F32),
            jax.ShapeDtypeStruct((seqs, rows, inner), BF16),
            jax.ShapeDtypeStruct((seqs, length, inner), BF16),
            jax.ShapeDtypeStruct((nz, seqs, length, width // nz), BF16),
            jax.ShapeDtypeStruct((seqs, state_width, inner), F32 if FINE_S else BF16),
            jax.ShapeDtypeStruct((8, inner), F32),
        ],
        scratch_shapes=[pltpu.VMEM((state_width, inner), F32)],
        compiler_params=pltpu.CompilerParams(vmem_limit_bytes=VMEM_ALL),
        name="mixed",
    )(ssd, v, gate_value, grad_inner, sums, OW, cum, carry, mat, ig, skip)


def backward_kernel(
    heads,
    gm_ref,
    v_ref,
    slope_ref,
    ssd_ref,
    starts_ref,
    carry_ref,
    cum_ref,
    step_ref,
    mat_ref,
    mslope_ref,
    start_ref,
    all_ref,
    ends_ref,
    gv_ref,
    small_ref,
    vk_ref,
    mk_ref,
    sb_ref,
    rate_ref,
    skip_ref,
    gx_ref,
    gs_ref,
    vec_ref,
    mvec_ref,
    svec_ref,
    incoming,
    ahead,
    mahead,
    step_dot,
    cum_grad,
    mixing,
    grad_b,
    grad_c,
    log_start,
):
    q, k = pl.program_id(0), pl.program_id(1)
    chunks = pl.num_programs(1)
    chunk = chunks - 1 - k
    mwidth = mk_ref.shape[1]
    half = mwidth // 2

    @pl.when(k == 0)
    def _():
        incoming[...] = join_states(all_ref, ends_ref, lax.axis_index("ctx"), True, 0)
        ahead[...] = jnp.zeros_like(ahead)
        mahead[...] = jnp.zeros_like(mahead)

    @pl.when((k == 0) & (q == 0))
    def _():
        vec_ref[...] = jnp.zeros_like(vec_ref)
        mvec_ref[...] = jnp.zeros_like(mvec_ref)
        svec_ref[...] = jnp.zeros_like(svec_ref)

    padded = pl.ds(pl.multiple_of(chunk * CHUNK, CHUNK), CHUNK + HALO)
    rows = pl.ds(pl.multiple_of(HALO + chunk * CHUNK, HALO), CHUNK)
    mat = mat_ref[0]
    b_mat, c_mat = mat[:, :half], mat[:, half:]
    b_low, c_low = b_mat.astype(BF16), c_mat.astype(BF16)
    ct_low = c_mat.T.astype(BF16)
    gram_t = dot_nt(b_low, c_low)
    step = step_ref[0]
    cum = cum_ref[0]
    cum_t = cum.T
    last = cum[CHUNK - 1 : CHUNK, :]
    from_start = jnp.exp(cum)
    to_end = jnp.exp(last - cum)
    whole = jnp.exp(last)
    before = jnp.exp(carry_ref[0, 0, 0:1, :])
    lane = iota(1)
    later = lane >= iota(0)

    step_dot[...] = jnp.zeros_like(step_dot)
    cum_grad[...] = jnp.zeros_like(cum_grad)
    mixing[...] = jnp.zeros_like(mixing)
    grad_b[...] = jnp.zeros_like(grad_b)
    grad_c[...] = jnp.zeros_like(grad_c)
    log_start[...] = jnp.zeros_like(log_start)

    for p in range(heads // 2):
        cols = slice(p * LANES, (p + 1) * LANES)
        gm = gm_ref[0, :, cols]
        v = v_ref[0, :, cols]
        stepped = pair(step, p)
        scaled = v * stepped
        gm_low, gm_rest = split(gm)
        scaled_low, scaled_rest = split(scaled)
        both = stacked(scaled_low.astype(F32))
        products = dot_nt(both, gm_low)
        if FINE_A:
            products = products + dot_nt(both, gm_rest)
            products = products + dot_nt(stacked(scaled_rest.astype(F32)), gm_low)
        weights = []
        mix = mixing[...]
        for i, h in enumerate((2 * p, 2 * p + 1)):
            spread = cum_t[h : h + 1, :] - cum[:, h : h + 1]
            decay = jnp.where(later, jnp.exp(spread), 0.0)
            weights.append(decay * gram_t)
            mix = mix + decay * products[i * CHUNK : (i + 1) * CHUNK]
        mixing[...] = mix
        weights = jnp.concatenate(weights, axis=1).astype(BF16)
        inc = incoming[:, cols]
        inc_low = inc.astype(BF16)
        ended = pair(to_end, p)
        b_dot = dot_nn(weights, stacked(gm)) + ended * dot_nn(b_low, inc_low)
        begun = gm * pair(from_start, p)
        begun_low = begun.astype(BF16)
        start = starts_ref[0, 0, :, cols] + pair(before, p) * start_ref[0, :, cols]
        if FINE_B:
            grad_b[...] += fine(dot_nt, scaled * ended, inc)
            grad_c[...] += fine(dot_nt, begun, start)
        else:
            grad_b[...] += dot_nt((scaled * ended).astype(BF16), inc_low)
            grad_c[...] += dot_nt(begun_low, start.astype(BF16))
        earlier = pair(whole, p) * inc + dot_nn(ct_low, begun_low)
        incoming[:, cols] = earlier
        heads_of = head_sums(p)
        log_start[...] += dot_nn(
            jnp.broadcast_to(jnp.sum(earlier * start, axis=0, keepdims=True), (8, LANES)),
            heads_of,
            HIGHEST,
        )
        step_dot[...] += dot_nn(v * b_dot, heads_of, HIGHEST)
        cum_grad[...] += dot_nn(
            gm_low.astype(F32) * ssd_ref[0, :, cols] - scaled.astype(BF16).astype(F32) * b_dot,
            heads_of,
            HIGHEST,
        )
        conv_grad = (stepped * b_dot + skip_ref[:, cols] * gm) * slope_ref[0, :, cols]
        taps = vk_ref[:, cols]
        width = taps.shape[0]
        signal = gv_ref[0, padded, cols].astype(F32)
        for offset in range(width):
            moved = signal if offset == width - 1 else pltpu.roll(signal, width - 1 - offset, 0)
            vec_ref[offset : offset + 1, cols] += jnp.sum(
                conv_grad * moved[HALO:], axis=0, keepdims=True
            )
        vec_ref[width : width + 1, cols] += jnp.sum(conv_grad, axis=0, keepdims=True)
        extended = jnp.concatenate([conv_grad, ahead[:, cols]], axis=0)
        gx_ref[0, rows, cols] = conv_back(extended, taps, CHUNK).astype(BF16)
        ahead[:, cols] = conv_grad[:HALO]

        @pl.when(chunk == 0)
        def _():
            front = jnp.concatenate([jnp.zeros((HALO, LANES), F32), conv_grad[:HALO]], axis=0)
            gx_ref[0, 0:HALO, cols] = conv_back(front, taps, HALO).astype(BF16)

    mix = mixing[...]
    if FINE_C:
        total_b = grad_b[...] + fine(dot_nn, mix, c_mat)
        total_c = grad_c[...] + fine(dot_nn, mix.T, b_mat)
    else:
        total_b = grad_b[...] + dot_nn(mix.astype(BF16), c_low)
        total_c = grad_c[...] + dot_nn(mix.T.astype(BF16), b_low)
    mgrad = jnp.concatenate([total_b, total_c], axis=1) * mslope_ref[0]
    mtaps = mk_ref[...]
    width = mtaps.shape[0]
    small = small_ref[0, padded, :]
    signal = small[:, :mwidth].astype(BF16).astype(F32)
    for offset in range(width):
        moved = signal if offset == width - 1 else pltpu.roll(signal, width - 1 - offset, 0)
        mvec_ref[offset : offset + 1, :] += jnp.sum(mgrad * moved[HALO:], axis=0, keepdims=True)
    mvec_ref[width : width + 1, :] += jnp.sum(mgrad, axis=0, keepdims=True)
    extended = jnp.concatenate([mgrad, mahead[...]], axis=0)
    gs_ref[0, rows, 0:mwidth] = conv_back(extended, mtaps, CHUNK).astype(BF16)
    mahead[...] = mgrad[:HALO]

    earlier_only = jnp.where(lane < iota(0), 1.0, 0.0)
    value_dot = step_dot[...]
    grad_log = log_start[0:1, :] - dot_nn(earlier_only, cum_grad[...], HIGHEST)
    grad_log = jnp.where(lane < heads, grad_log, 0.0)
    grad_step = value_dot + grad_log * rate_ref[...]
    raw = small[HALO:, mwidth:] + sb_ref[...]
    grad_raw = jnp.where(lane < heads, grad_step * sigmoid(raw), 0.0)
    svec_ref[0:1, :] += jnp.sum(grad_raw, axis=0, keepdims=True)
    svec_ref[1:2, :] += jnp.sum(grad_log * step, axis=0, keepdims=True)
    gs_ref[0, rows, mwidth:] = grad_raw.astype(BF16)

    @pl.when(chunk == 0)
    def _():
        front = jnp.concatenate([jnp.zeros((HALO, mwidth), F32), mgrad[:HALO]], axis=0)
        gs_ref[0, 0:HALO, 0:mwidth] = conv_back(front, mtaps, HALO).astype(BF16)
        gs_ref[0, 0:HALO, mwidth:] = jnp.zeros((HALO, gs_ref.shape[2] - mwidth), BF16)


def backward(
    gm, v, slope, ssd, starts, carry, cum, step, mat, mslope, start, adjoints, ends,
    gate_value, small, vk, mk, sb, rate, skip, heads,
):
    seqs, length, inner = gm.shape
    rows = gate_value.shape[1]
    chunks = length // CHUNK
    state_width = mat.shape[2] // 2
    count = adjoints.shape[0]
    swidth = small.shape[2]
    full = lambda array: pl.BlockSpec(array.shape, lambda q, k: (0, 0))
    tile = lambda cols: pl.BlockSpec((1, CHUNK, cols), lambda q, k: (q, chunks - 1 - k, 0))
    whole = lambda height, cols, at=0: pl.BlockSpec((1, height, cols), lambda q, k: (q, 0, at))
    every = lambda height, cols: pl.BlockSpec((count, 1, height, cols), lambda q, k: (0, q, 0, 0))
    return pl.pallas_call(
        functools.partial(backward_kernel, heads),
        grid=(seqs, chunks),
        in_specs=[
            tile(inner),
            tile(inner),
            tile(inner),
            tile(inner),
            pl.BlockSpec((1, 1, state_width, inner), lambda q, k: (q, chunks - 1 - k, 0, 0)),
            pl.BlockSpec((1, 1, 8, LANES), lambda q, k: (q, chunks - 1 - k, 0, 0)),
            tile(LANES),
            tile(LANES),
            tile(2 * state_width),
            tile(2 * state_width),
            whole(state_width, inner),
            every(state_width, inner),
            every(8, inner),
            whole(rows, inner, 1),
            whole(rows, swidth),
            full(vk),
            full(mk),
            full(sb),
            full(rate),
            full(skip),
        ],
        out_specs=[
            whole(rows, inner),
            whole(rows, swidth),
            pl.BlockSpec((8, inner), lambda q, k: (0, 0)),
            pl.BlockSpec((8, 2 * state_width), lambda q, k: (0, 0)),
            pl.BlockSpec((8, LANES), lambda q, k: (0, 0)),
        ],
        out_shape=[
            jax.ShapeDtypeStruct((seqs, rows, inner), BF16),
            jax.ShapeDtypeStruct((seqs, rows, swidth), BF16),
            jax.ShapeDtypeStruct((8, inner), F32),
            jax.ShapeDtypeStruct((8, 2 * state_width), F32),
            jax.ShapeDtypeStruct((8, LANES), F32),
        ],
        scratch_shapes=[
            pltpu.VMEM((state_width, inner), F32),
            pltpu.VMEM((HALO, inner), F32),
            pltpu.VMEM((HALO, 2 * state_width), F32),
        ]
        + [pltpu.VMEM((CHUNK, LANES), F32)] * 5
        + [pltpu.VMEM((8, LANES), F32)],
        compiler_params=pltpu.CompilerParams(vmem_limit_bytes=VMEM_ALL),
        name="backward",
    )(
        gm, v, slope, ssd, starts, carry, cum, step, mat, mslope, start, adjoints, ends,
        gate_value, small, vk, mk, sb, rate, skip,
    )


def normed_kernel(blocks, gz_ref, gx_ref, gs_ref, normed_ref, gv_ref, sw_ref, out_ref, row_ref, col_ref, acc):
    q = pl.program_id(0)
    height = gz_ref.shape[1] // blocks
    inner = gz_ref.shape[2]
    width = out_ref.shape[2]

    @pl.when(q == 0)
    def _():
        col_ref[...] = jnp.zeros_like(col_ref)

    acc[...] = jnp.zeros_like(acc)
    for r in range(blocks):
        rows = slice(r * height, (r + 1) * height)
        part = dot_nt(gz_ref[0, rows, :], gv_ref[:, 0:inner])
        part = part + dot_nt(gx_ref[0, rows, :], gv_ref[:, inner:])
        part = part + dot_nt(gs_ref[0, rows, :], sw_ref[...])
        out_ref[0, rows, :] = part.astype(BF16)
        product = part * normed_ref[0, rows, :].astype(F32)
        col_ref[0:1, :] += jnp.sum(product, axis=0, keepdims=True)
        total = product[:, 0:LANES]
        for t in range(1, width // LANES):
            total = total + product[:, t * LANES : (t + 1) * LANES]
        acc[rows, :] = total
    row_ref[0] = dot_nt(jnp.ones((8, LANES), F32), acc[...], HIGHEST)


def normed_grad(gz, gx, gs, normed, GV, SW):
    seqs, rows, width = normed.shape
    padded = -(-rows // LANES) * LANES
    full = lambda array: pl.BlockSpec(array.shape, lambda q: (0, 0))
    tile = lambda array: pl.BlockSpec((1,) + array.shape[1:], lambda q: (q, 0, 0))
    return pl.pallas_call(
        functools.partial(normed_kernel, 3),
        grid=(seqs,),
        in_specs=[tile(gz), tile(gx), tile(gs), tile(normed), full(GV), full(SW)],
        out_specs=[
            tile(normed),
            pl.BlockSpec((1, 8, padded), lambda q: (q, 0, 0)),
            pl.BlockSpec((8, width), lambda q: (0, 0)),
        ],
        out_shape=[
            jax.ShapeDtypeStruct((seqs, rows, width), BF16),
            jax.ShapeDtypeStruct((seqs, 8, padded), F32),
            jax.ShapeDtypeStruct((8, width), F32),
        ],
        scratch_shapes=[pltpu.VMEM((padded, LANES), F32)],
        compiler_params=pltpu.CompilerParams(vmem_limit_bytes=VMEM_ALL),
        name="normed_grad",
    )(gz, gx, gs, normed, GV, SW)


def reduce_kernel(dims, mwidth, *refs):
    ns, nc, nz = dims
    s, c, z = places()
    part, rowsum, vec, zvec = refs[:4]
    grads = refs[4:8]
    out_part, out_row, out_vec, out_zvec = refs[8:12]
    out_grads = refs[12:16]
    up_buf, down_buf, halo_buf, row_buf, row_halo = refs[16:21]
    shard_bufs = refs[21:25]
    ctx_bufs = refs[25:29]
    mat_own, mat_buf, vec_c, vec_own, vec_s, zvec_c, zvec_own, zvec_s, zvec_z = refs[29:38]
    (us, ur, ds_, dr, hs, hr, rs, rr, rhs, rhr, ss, sr, cs, cr, ms, mr, vcs, vcr, vss, vsr, vzs, vzr) = refs[38:]
    seqs, rows, width = part.shape
    quarter = width // nz
    first_rows = rows // 2 // HALO * HALO + (HALO if (rows // HALO) % 2 else 0)
    spans = [(0, first_rows), (first_rows, rows - first_rows)]
    parts = [(q, r0, n) for q in range(seqs) for r0, n in spans]

    peers = [(None, {"tensor": lax.rem(z + k, nz)}) for k in range(1, nz)]
    peers += [(None, {"ctx": lax.rem(c + k, nc)}) for k in range(1, nc)]
    peers += [(None, {"shard": lax.rem(s + j, ns)}) for j in range(1, ns)]
    greet(peers, (nz - 1) + (nc - 1) + (ns - 1))

    def own(i, j):
        q, r0, n = parts[i]
        return part.at[q, pl.ds(r0, n), pl.ds(j * quarter, quarter)]

    def slot(buf, i, j):
        q, r0, n = parts[i]
        return buf.at[j, q, pl.ds(r0, n), :]

    def up(i, j, first):
        src = own(i, j) if first else slot(up_buf, i, j)
        return remote(src, slot(up_buf, i, j), us.at[j, i], ur.at[j, i], tensor=lax.rem(z + 1, nz))

    def down(i, j, first):
        src = own(i, j) if first else slot(down_buf, i, j)
        return remote(
            src, slot(down_buf, i, j), ds_.at[j, i], dr.at[j, i], tensor=lax.rem(z + nz - 1, nz)
        )

    def to_shard(j, a):
        peer = lax.rem(s + j, ns)
        n = grads[a].shape[0] // ns
        src = grads[a].at[pl.ds(pl.multiple_of(peer * n, n), n), :]
        return remote(src, shard_bufs[a].at[j - 1], ss.at[j - 1, a], sr.at[j - 1, a], shard=peer)

    for a in (3, 0, 1, 2):
        for j in range(1, ns):
            to_shard(j, a).start()

    for j in reversed(range(1, nz)):
        for i in range(len(parts)):

            @pl.when(z == 0)
            def _():
                up(i, j, True).start()

            @pl.when(z == nz - 1)
            def _():
                down(i, nz - 1 - j, True).start()

    def row_send(k):
        return remote(rowsum, row_buf.at[k - 1], rs.at[k - 1], rr.at[k - 1], tensor=lax.rem(z + k, nz))

    def vec_ctx(k, b):
        src, dst = ((vec, vec_c), (zvec, zvec_c))[b]
        return remote(src, dst.at[k - 1], vcs.at[k - 1, b], vcr.at[k - 1, b], ctx=lax.rem(c + k, nc))

    def vec_shard(j, b):
        src, dst = ((vec_own, vec_s), (zvec_own, zvec_s))[b]
        return remote(src, dst.at[j - 1], vss.at[j - 1, b], vsr.at[j - 1, b], shard=lax.rem(s + j, ns))

    def vec_z(k):
        return remote(out_zvec, zvec_z.at[k - 1], vzs.at[k - 1], vzr.at[k - 1], tensor=lax.rem(z + k, nz))

    for k in range(1, nz):
        row_send(k).start()
    for k in range(1, nc):
        for b in range(2):
            vec_ctx(k, b).start()

    row_back = remote(
        out_row.at[:, :, pl.ds(0, LANES)], row_halo, rhs, rhr, ctx=lax.rem(c + nc - 1, nc)
    )

    def rows_step():
        total = rowsum[...]
        for k in range(1, nz):
            row_send(k).wait_recv()
            total = total + row_buf[k - 1]
        out_row[...] = total

        @pl.when(c > 0)
        def _():
            row_back.start()

    def vec_step():
        for b in range(2):
            src, dst, slots = ((vec, vec_own, vec_c), (zvec, zvec_own, zvec_c))[b]
            total = src[...]
            for k in range(1, nc):
                vec_ctx(k, b).wait_recv()
                total = total + slots[k - 1]
            dst[...] = total
            for j in range(1, ns):
                vec_shard(j, b).start()

    def vec_next():
        for b in range(2):
            src, dst, slots = ((vec_own, out_vec, vec_s), (zvec_own, out_zvec, zvec_s))[b]
            total = src[...]
            for j in range(1, ns):
                vec_shard(j, b).wait_recv()
                total = total + slots[j - 1]
            dst[...] = total
        for k in range(1, nz):
            vec_z(k).start()

    def to_ctx(k, a):
        peer = lax.rem(c + k, nc)
        n = out_grads[a].shape[0]
        src = shard_bufs[a].at[0, pl.ds(pl.multiple_of(peer * n, n), n), :]
        return remote(src, ctx_bufs[a].at[k - 1], cs.at[k - 1, a], cr.at[k - 1, a], ctx=peer)

    def shard_step(a):
        n = out_grads[a].shape[0]
        for j in range(1, ns):
            to_shard(j, a).wait_recv()

        for k in list(range(1, nc)) + [0]:
            block = lax.rem(c + k, nc)
            there = pl.ds(pl.multiple_of(block * n, n), n)
            mine = pl.ds(pl.multiple_of((s * nc + block) * n, n), n)
            total = grads[a][mine, :].astype(F32)
            for j in range(1, ns):
                total = total + shard_bufs[a][j - 1, there, :].astype(F32)
            if k == 0:
                out_grads[a][...] = total
            else:
                shard_bufs[a][0, there, :] = total.astype(BF16)
                to_ctx(k, a).start()

    def ctx_step(a):
        for k in range(1, nc):
            to_ctx(k, a).wait_recv()
        total = out_grads[a][...]
        for k in range(1, nc):
            total = total + ctx_bufs[a][k - 1].astype(F32)
        out_grads[a][...] = total

    def line_step(j, i):
        q, r0, n = parts[i]
        t = nz - 1 - j

        @pl.when((z > 0) & (z < j))
        def _():
            up(i, j, False).wait_recv()
            up_buf[j, q, r0 : r0 + n, :] = (
                up_buf[j, q, r0 : r0 + n, :].astype(F32)
                + part[q, r0 : r0 + n, j * quarter : (j + 1) * quarter].astype(F32)
            ).astype(BF16)
            up(i, j, False).start()

        @pl.when((z < nz - 1) & (z > t))
        def _():
            down(i, t, False).wait_recv()
            down_buf[t, q, r0 : r0 + n, :] = (
                down_buf[t, q, r0 : r0 + n, :].astype(F32)
                + part[q, r0 : r0 + n, t * quarter : (t + 1) * quarter].astype(F32)
            ).astype(BF16)
            down(i, t, False).start()

    line = [
        functools.partial(line_step, j, i) for j in reversed(range(2, nz)) for i in range(len(parts))
    ]
    others = [functools.partial(shard_step, a) for a in (3, 0, 1, 2)] + [rows_step, vec_step, vec_next]
    for i in range(max(len(line), len(others))):
        if i < len(line):
            line[i]()
        if i < len(others):
            others[i]()
    ctx_step(3)
    mat_own[...] = out_grads[3][:, 0:mwidth].astype(BF16)

    def mat_send(k):
        return remote(
            mat_own, mat_buf.at[k - 1], ms.at[k - 1], mr.at[k - 1], tensor=lax.rem(z + k, nz)
        )

    for k in range(1, nz):
        mat_send(k).start()
    for a in range(3):
        ctx_step(a)
    for j in range(nz):
        for i in range(len(parts)):

            @pl.when((z == j) & (z > 0))
            def _():
                up(i, j, False).wait_recv()

            @pl.when((z == j) & (z < nz - 1))
            def _():
                down(i, j, False).wait_recv()

    mine = pl.ds(pl.multiple_of(z * quarter, quarter), quarter)
    out_part[...] = part[:, :, mine].astype(F32)

    @pl.when(z > 0)
    def _():
        out_part[...] += up_buf[z].astype(F32)

    @pl.when(z < nz - 1)
    def _():
        out_part[...] += down_buf[z].astype(F32)

    halo = remote(
        out_part.at[:, pl.ds(0, HALO), :], halo_buf, hs, hr, ctx=lax.rem(c + nc - 1, nc)
    )

    @pl.when(c > 0)
    def _():
        halo.start()

    total = out_grads[3][:, 0:mwidth]
    for k in range(1, nz):
        mat_send(k).wait_recv()
        total = total + mat_buf[k - 1].astype(F32)
    out_grads[3][:, 0:mwidth] = total
    vec_sum = out_zvec[...]
    for k in range(1, nz):
        vec_z(k).wait_recv()
        vec_sum = vec_sum + zvec_z[k - 1]
    for k in range(1, nz):
        vec_z(k).wait_send()
    out_zvec[...] = vec_sum

    @pl.when(c > 0)
    def _():
        row_back.wait_send()
        halo.wait_send()

    @pl.when(c < nc - 1)
    def _():
        row_back.wait_recv()
        tail = slice(rows - HALO, rows - HALO + LANES)
        out_row[:, :, tail] += row_halo[...]
        halo.wait_recv()
        out_part[:, rows - HALO :, :] += halo_buf[...]

    for j in reversed(range(1, nz)):
        for i in range(len(parts)):
            t = nz - 1 - j

            @pl.when(z < j)
            def _():
                up(i, j, False).wait_send()

            @pl.when(z > t)
            def _():
                down(i, t, False).wait_send()

    for a in range(4):
        for j in range(1, ns):
            to_shard(j, a).wait_send()
        for k in range(1, nc):
            to_ctx(k, a).wait_send()
    for k in range(1, nz):
        row_send(k).wait_send()
        mat_send(k).wait_send()
    for b in range(2):
        for k in range(1, nc):
            vec_ctx(k, b).wait_send()
        for j in range(1, ns):
            vec_shard(j, b).wait_send()


def reduce_all(part, rowsum, vec, zvec, grads, mwidth):
    ns, nc, nz = dims = sizes()
    seqs, rows, width = part.shape
    quarter = width // nz
    own = [(g.shape[0] // (ns * nc), g.shape[1]) for g in grads]
    dma = pltpu.SemaphoreType.DMA
    halves = 2 * seqs
    shape = jax.ShapeDtypeStruct
    buffers = [
        pltpu.VMEM((nz, seqs, rows, quarter), BF16),
        pltpu.VMEM((nz, seqs, rows, quarter), BF16),
        pltpu.VMEM((seqs, HALO, quarter), F32),
        pltpu.VMEM((nz - 1,) + rowsum.shape, F32),
        pltpu.VMEM(rowsum.shape[:2] + (LANES,), F32),
    ]
    buffers += [pltpu.VMEM((ns - 1, g.shape[0] // ns, g.shape[1]), BF16) for g in grads]
    buffers += [pltpu.VMEM((nc - 1,) + o, BF16) for o in own]
    block = own[3][0]
    buffers += [
        pltpu.VMEM((block, mwidth), BF16),
        pltpu.VMEM((nz - 1, block, mwidth), BF16),
        pltpu.VMEM((nc - 1,) + vec.shape, F32),
        pltpu.VMEM(vec.shape, F32),
        pltpu.VMEM((ns - 1,) + vec.shape, F32),
        pltpu.VMEM((nc - 1,) + zvec.shape, F32),
        pltpu.VMEM(zvec.shape, F32),
        pltpu.VMEM((ns - 1,) + zvec.shape, F32),
        pltpu.VMEM((nz - 1,) + zvec.shape, F32),
    ]
    semaphores = [dma((nz, halves))] * 4 + [dma] * 2 + [dma((nz - 1,))] * 2 + [dma] * 2
    semaphores += [dma((ns - 1, 4))] * 2 + [dma((nc - 1, 4))] * 2 + [dma((nz - 1,))] * 2
    semaphores += [dma((nc - 1, 2))] * 2 + [dma((ns - 1, 2))] * 2 + [dma((nz - 1,))] * 2
    return pl.pallas_call(
        functools.partial(reduce_kernel, dims, mwidth),
        out_shape=[
            shape((seqs, rows, quarter), F32),
            shape(rowsum.shape, F32),
            shape(vec.shape, F32),
            shape(zvec.shape, F32),
        ]
        + [shape(o, F32) for o in own],
        in_specs=[vmem_spec()] * 8,
        out_specs=[vmem_spec()] * 8,
        scratch_shapes=buffers + semaphores,
        compiler_params=pltpu.CompilerParams(
            collective_id=4, has_side_effects=True, vmem_limit_bytes=VMEM_ALL
        ),
        name="reduce_all",
    )(part, rowsum, vec, zvec, *grads)


def body(
    block_input,
    output_cotangent,
    norm_gain,
    gate_value_weight,
    matrix_weight,
    step_weight,
    out_weight,
    value_kernel,
    value_bias,
    matrix_kernel,
    matrix_bias,
    step_bias,
    decay_log,
    skip_gain,
    inner_gain,
):
    seqs, length, quarter = block_input.shape
    heads = step_bias.shape[0]
    inner = inner_gain.shape[0]
    head_width = inner // heads
    mwidth = matrix_weight.shape[1]
    block = matrix_weight.shape[0]
    ns, nc, nz = sizes()
    inner_total = inner * nz
    model_width = quarter * nz

    small_weight = jnp.concatenate(
        [
            matrix_weight,
            step_weight,
            norm_gain[:, None],
            jnp.zeros((block, LANES - heads - 1), BF16),
        ],
        axis=1,
    )
    X, GV, OW, SW = gather(
        block_input, gate_value_weight.reshape(block, 2 * inner), out_weight, small_weight
    )
    gain = SW[:, mwidth + heads].astype(F32).reshape(1, model_width)
    cot_late, X = lax.optimization_barrier((output_cotangent, X))
    full_cot = lax.all_gather(cot_late, "tensor", axis=2, tiled=True)

    lane_row = lambda array: jnp.pad(array, (0, LANES - heads))[None, :]
    rate_heads = -jnp.exp(decay_log)
    rate, sb = lane_row(rate_heads), lane_row(step_bias)
    skip = jnp.repeat(skip_gain, head_width)[None, :]
    ig = inner_gain[None, :]

    normed, gate_value, small, scale = project(X, gain, GV, SW)
    v, slope, y, starts, own, step, cum, carry, mat, mslope, end = forward(
        gate_value,
        small,
        value_kernel,
        value_bias[None, :],
        matrix_kernel,
        matrix_bias[None, :],
        sb,
        rate,
        heads,
    )
    states, ends = exchange(own, end, False)
    ssd, grad_inner, sums, start = gate_step(
        y, v, gate_value, full_cot, OW, cum, carry, mat, states, ends, ig, skip, heads
    )
    sums = token_sum(sums)
    gm, gz, normed_inner, part, adjoint, gvec = mixed_step(
        ssd, v, gate_value, grad_inner, sums, OW, cum, carry, mat, ig, skip, heads, inner_total, nz
    )
    share = lax.psum_scatter(part, "tensor", scatter_dimension=0, tiled=True)[0]
    block_output = (block_input.astype(F32) + share.astype(F32)).astype(BF16)
    adjoints, _ = exchange(adjoint, end, True)
    gx, gs, bvec, mvec, svec = backward(
        gm, v, slope, ssd, starts, carry, cum, step, mat, mslope, start, adjoints, ends,
        gate_value, small, value_kernel, matrix_kernel, sb, rate, skip, heads,
    )
    grad_part, rowsum, colsum = normed_grad(gz, gx, gs, normed, GV, SW)
    grads = (
        dot_tokens(normed, gz).astype(BF16),
        dot_tokens(normed, gx).astype(BF16),
        dot_tokens(full_cot, normed_inner).astype(BF16),
        dot_tokens(normed, gs).astype(BF16),
    )
    kernel_width = value_kernel.shape[0]
    tail = jnp.concatenate(
        [
            svec[0, :heads],
            rate_heads * svec[1, :heads],
            jnp.sum(gvec[1].reshape(heads, head_width), axis=1),
            jnp.zeros((inner - 3 * heads,), F32),
        ]
    )
    vec = jnp.concatenate(
        [
            bvec[: kernel_width + 1],
            gvec[0:1],
            tail[None, :],
            jnp.zeros((8 - kernel_width - 3, inner), F32),
        ],
        axis=0,
    )
    norm_part = colsum[0] / gain[0]
    flat = jnp.concatenate([mvec[: kernel_width + 1].reshape(-1), norm_part])
    zlanes = -(-flat.shape[0] // (8 * LANES)) * LANES
    zvec = jnp.pad(flat, (0, 8 * zlanes - flat.shape[0])).reshape(8, zlanes)

    grad_quarter, row_total, vec, zvec, gz_w, gx_w, ow_w, small_w = reduce_all(
        grad_part, rowsum, vec, zvec, grads, mwidth
    )
    z = lax.axis_index("tensor")
    feature = z * quarter
    gain_quarter = lax.dynamic_slice_in_dim(gain[0], feature, quarter, axis=0)
    scale_own = scale[:, HALO:, :1]
    normal = block_input.astype(F32) * scale_own
    row_mean = row_total[:, 0, HALO : HALO + length] / model_width
    input_grad = scale_own * (
        grad_quarter[:, HALO:] * gain_quarter - normal * row_mean[:, :, None]
    ) + output_cotangent.astype(F32)
    flat = zvec.reshape(-1)
    msize = (kernel_width + 1) * mwidth
    mgrads = flat[:msize].reshape(kernel_width + 1, mwidth)
    place = (lax.axis_index("shard") * nc + lax.axis_index("ctx")) * block
    norm_grad = lax.dynamic_slice_in_dim(flat[msize : msize + model_width], place, block, axis=0)
    tail = vec[kernel_width + 2]
    return (
        block_output,
        input_grad,
        norm_grad,
        jnp.stack([gz_w, gx_w], axis=1),
        small_w[:, :mwidth],
        small_w[:, mwidth : mwidth + heads],
        ow_w,
        vec[:kernel_width],
        vec[kernel_width],
        mgrads[:kernel_width],
        mgrads[kernel_width],
        tail[:heads],
        tail[heads : 2 * heads],
        tail[2 * heads : 3 * heads],
        vec[kernel_width + 1],
    )


def solution(mesh):
    placed = (
        P("shard", "ctx", "tensor"),
        P("shard", "ctx", "tensor"),
        P(("shard", "ctx")),
        P(("shard", "ctx"), None, "tensor"),
        P(("shard", "ctx"), None),
        P(("shard", "ctx"), "tensor"),
        P(("shard", "ctx"), "tensor"),
        P(None, "tensor"),
        P("tensor"),
        P(),
        P(),
        P("tensor"),
        P("tensor"),
        P("tensor"),
        P("tensor"),
    )
    return jax.shard_map(
        body,
        mesh=mesh,
        in_specs=placed,
        out_specs=(
            P("shard", "ctx", "tensor"),
            P("shard", "ctx", "tensor"),
            P(("shard", "ctx")),
            P(("shard", "ctx"), None, "tensor"),
            P(("shard", "ctx"), None),
            P(("shard", "ctx"), "tensor"),
            P(("shard", "ctx"), "tensor"),
            P(None, "tensor"),
            P("tensor"),
            P(),
            P(),
            P("tensor"),
            P("tensor"),
            P("tensor"),
            P("tensor"),
        ),
        check_vma=False,
    )
```

time: 1000 us -> 421 us (0.42)
  waiting for transfers between devices: 380 us -> 0.06 us
  Pallas kernels: 0 us -> 351 us
  blocking collectives: 151 us -> 0 us
  local copies, waits for them, and re-layouts: 169 us -> 24.1 us
  matrix products: 155 us -> 18.4 us
  other arithmetic: 114 us -> 11.2 us
    pallas_call x0 -> x11, Pallas kernels: none -> 351 us  [the longest x1 90 us: reduce_all(): pl.pallas_call(functools.partial(reduce_kernel, dims, mwidth), out_shape=...]
    reduce_scatter x4 -> x1, waiting for transfers between devices: 251 us -> 0.01 us  [body(): share = lax.psum_scatter(part, 'tensor', scatter_dimension=0, tiled=True)[0]]
    dot_general x36 -> x4, matrix products: 142 us -> 18.4 us  [dot_tokens(): lax.dot_general(left, right, ((axes, axes), ((), ())), preferred_element_...]
    unnamed x3 -> x0, blocking collectives: 68.6 us -> none
    all_gather x6 -> x1, waiting for transfers between devices: 67.3 us -> 0.02 us  [body(): full_cot = lax.all_gather(cot_late, 'tensor', axis=2, tiled=True)]
    all_gather x3 -> x0, blocking collectives: 62.5 us -> none  [the longest x1 28.6 us: body(): lax.all_gather(matrix_weight, ('shard', 'ctx'), axis=0, tiled=True)]
    unnamed x15 -> x2, waiting for transfers between devices: 57.1 us -> 0.03 us
    reduce_sum x10 -> x1, other arithmetic: 39.5 us -> 0.12 us  [body(): jnp.sum(gvec[1].reshape(heads, head_width), axis=1)]
  transfers between devices with their start and end apart: 15 -> 2, of which waited for: 9 -> 0; matrix products, arithmetic and copies ran while one was open for 27% -> 11% of each run, Pallas kernels for 0% -> 60%
where the time goes in v1:
time: 421 us; the launch traced here: 420 us
  Pallas kernels  351 us (83%)
  local copies, waits for them, and re-layouts  24.1 us (6%)
  matrix products  18.4 us (4%)
  between operations  14.3 us (3%)
  other arithmetic  11.2 us (3%)
    pallas_call x1, Pallas kernels, reduce_all(): pl.pallas_call(functools.partial(reduce_kernel, dims, mwidth), out_shape=...  90 us
    pallas_call x2, Pallas kernels, exchange(): pl.pallas_call(functools.partial(exchange_kernel, dims, backward), out_sh...  76 us
    pallas_call x1, Pallas kernels, gather(): pl.pallas_call(functools.partial(gather_kernel, dims), out_shape=[jax.Sha...  60.6 us
    pallas_call x1, Pallas kernels, backward(): pl.pallas_call(functools.partial(backward_kernel, heads), grid=(seqs, chu...  41.4 us
    dot_general x4, matrix products, dot_tokens(): lax.dot_general(left, right, ((axes, axes), ((), ())), preferred_element_...  18.4 us
    pallas_call x1, Pallas kernels, normed_grad(): pl.pallas_call(functools.partial(normed_kernel, 3), grid=(seqs,), in_spec...  17.6 us
    pallas_call x1, Pallas kernels, mixed_step(): pl.pallas_call(functools.partial(mixed_kernel, heads, inner_total), grid=...  16.6 us
    pallas_call x1, Pallas kernels, forward(): pl.pallas_call(functools.partial(forward_kernel, heads), grid=(seqs, chun...  15.5 us
  transfers between devices with their start and end apart: 2, of which 0 were waited for; matrix products, arithmetic and copies ran while one was open for 11% of the time, Pallas kernels for 60%

profile of v1, /device:TPU:0, one launch (start us, length us, event | category | flops | bytes accessed | tf_op | source)
XLA Modules:
  0.0 419.5 jit_solution(14231017949013046364)
XLA Ops:
  8.0 0.8 copy.34
  8.8 1.9 copy.41
  10.8 1.6 maximum_maximum_fusion.sw_ref
  12.5 60.6 %gather.1 = (bf16[2,528,1536]{2,1,0:T(8,128)(2,1)}, bf16[1536,1536]{1,0:T(8,128)(2,1)}, bf16[1536,768]{1,0:T(8,128)(2,1)}, bf16[1536,384]{1,0:T(8,128)(2,1)}) custom-call(bf16[2,512,384]{2,1,0:T(8,128)(2,1)} %x_ref.1, bf16[192,1536]{1,0:T(8,128)(2,1)} %bitcast.46, bf16[192,768]{1,0:T(8,128)(2,1)} %ow_ref.1, bf16[192,384]{1,0:T(8,128)(2,1)} %maximum_maximum_fusion.sw_ref), custom_call_target="tpu_custom_call" | custom-call | tf_op jit(solution)/shard_map/gather/pallas_call | solution.py:289
  75.1 1.3 fusion.6
  77.0 12.6 %project.1 = (bf16[2,528,1536]{2,1,0:T(8,128)(2,1)}, bf16[2,528,1536]{2,1,0:T(8,128)(2,1)}, f32[2,528,384]{2,1,0:T(8,128)}, f32[2,528,128]{2,1,0:T(8,128)}) custom-call(bf16[2,528,1536]{2,1,0:T(8,128)(2,1)} %get-tuple-element.66.x_ref, f32[1,1536]{1,0:T(1,128)} %reshape.81.gain_ref, bf16[1536,1536]{1,0:T(8,128)(2,1)} %get-tuple-element.68.gv_ref, ...), custom_call_target="tpu_custom_call" | custom-call | tf_op jit(solution)/shard_map/project/pallas_call | solution.py:328
  90.2 15.5 %forward.1 = (f32[2,512,768]{2,1,0:T(8,128)}, f32[2,512,768]{2,1,0:T(8,128)}, f32[2,512,768]{2,1,0:T(8,128)}, f32[2,4,128,768]{3,2,1,0:T(8,128)}, f32[2,128,768]...) custom-call(bf16[2,528,1536]{2,1,0:T(8,128)(2,1)} %get-tuple-element, ...), custom_call_target="tpu_custom_call" | custom-call | tf_op jit(solution)/shard_map/forward/pallas_call | solution.py:525
  105.7 37.5 %states.1 = (f32[4,2,128,768]{3,2,1,0:T(8,128)}, f32[4,2,8,768]{3,2,1,0:T(8,128)}) custom-call(f32[2,128,768]{2,1,0:T(8,128)} %get-tuple-element.78.own_ref, f32[2,8,768]{2,1,0:T(8,128)} %get-tuple-element.79.end_ref), custom_call_target="tpu_custom_call" | custom-call | tf_op jit(solution)/shard_map/states/pallas_call | solution.py:607
  143.2 13.7 %gates.1 = (f32[2,512,768]{2,1,0:T(8,128)}, f32[2,512,768]{2,1,0:T(8,128)}, f32[2,8,512]{2,1,0:T(8,128)}, f32[2,128,768]{2,1,0:T(8,128)}) custom-call(f32[2,512,768]{2,1,0:T(8,128)} %get-tuple-element.71.y_ref, f32[2,512,768]{2,1,0:T(8,128)} %get-tuple-element.72.v_ref, bf16[2,528,1536]{2,1,0:T(8,128)(2,1)} %get-tuple-element.69.gv_ref, ...), custom_call_target="tpu_custom_call" | custom-call | tf_op jit(solution)/shard_map/gates/pallas_call | solution.py:679
  156.9 7.2 %token_sum.1.sums_ref = f32[2,8,512]{2,1,0:T(8,128)} custom-call(f32[2,8,512]{2,1,0:T(8,128)} %get-tuple-element.84.own_ref), custom_call_target="tpu_custom_call" | custom-call | tf_op jit(solution)/shard_map/token_sum/pallas_call | solution.py:737
  164.2 16.6 %mixed.1 = (f32[2,512,768]{2,1,0:T(8,128)}, bf16[2,528,768]{2,1,0:T(8,128)(2,1)}, bf16[2,512,768]{2,1,0:T(8,128)(2,1)}, bf16[4,2,512,384]{3,2,1,0:T(8,128)(2,1)}...) custom-call(f32[2,512,768]{2,1,0:T(8,128)} %get-tuple-element.82.ssd_ref, f32[2,512,768]{2,1,0:T(8,128)} %get-tuple-element.72.v_ref, ...), custom_call_target="tpu_custom_call" | custom-call | tf_op jit(solution)/shard_map/mixed/pallas_call | solution.py:829
  180.9 1.2 slice_convert_fusion
  182.5 0.8 fusion.7
  183.5 38.5 %adjoints.1 = (f32[4,2,128,768]{3,2,1,0:T(8,128)}, f32[4,2,8,768]{3,2,1,0:T(8,128)}) custom-call(f32[2,128,768]{2,1,0:T(8,128)} %get-tuple-element.94.own_ref, f32[2,8,768]{2,1,0:T(8,128)} %get-tuple-element.79.end_ref), custom_call_target="tpu_custom_call" | custom-call | tf_op jit(solution)/shard_map/adjoints/pallas_call | solution.py:607
  222.0 41.4 %backward.1 = (bf16[2,528,768]{2,1,0:T(8,128)(2,1)}, bf16[2,528,384]{2,1,0:T(8,128)(2,1)}, f32[8,768]{1,0:T(8,128)}, f32[8,256]{1,0:T(8,128)}, f32[8,128]{1,0:T(8,128)}) custom-call(f32[2,512,768]{2,1,0:T(8,128)} %get-tuple-element.88.gm_ref, f32[2,512,768]{2,1,0:T(8,128)} %get-tuple-element.72.v_ref, f32[2,512,768]{2,1,0:T(8,128)} %get-tuple-element.89.slope_ref, ...), custom_call_target="tpu_custom_call" | custom-call | tf_op jit(solution)/shard_map/backward/pallas_call | solution.py:1067
  265.6 17.6 %normed_grad.1 = (bf16[2,528,1536]{2,1,0:T(8,128)(2,1)}, f32[2,8,640]{2,1,0:T(8,128)}, f32[8,1536]{1,0:T(8,128)}) custom-call(bf16[2,528,768]{2,1,0:T(8,128)(2,1)} %get-tuple-element.87.gz_ref, bf16[2,528,768]{2,1,0:T(8,128)(2,1)} %get-tuple-element.96.gx_ref, bf16[2,528,384]{2,1,0:T(8,128)(2,1)} %get-tuple-element.97.gs_ref, ...), custom_call_target="tpu_custom_call" | custom-call | tf_op jit(solution)/shard_map/normed_grad/pallas_call | solution.py:1152
  283.2 0.8 slice_reduce_fusion.1
  285.3 5.2 %fusion.refs_7_ = bf16[1536,384]{1,0:T(8,128)(2,1)} fusion(bf16[2,528,1536]{2,1,0:T(8,128)(2,1)} %get-tuple-element.98.normed_ref, bf16[2,528,384]{2,1,0:T(8,128)(2,1)S(1)} %copy-done.7), kind=kOutput, calls=%fused_computation.4 | convolution fusion | flops 1246298112 | bytes 5234688 | tf_op jit(solution)/shard_map/dot_general | solution.py:39
  290.6 4.0 bitcast_convert_fusion.refs_6_
  294.6 4.6 %bitcast_convert_fusion.2.refs_4_ = bf16[1536,768]{1,0:T(8,128)(2,1)} fusion(bf16[2,528,1536]{2,1,0:T(8,128)(2,1)S(1)} %copy-done, bf16[2,528,768]{2,1,0:T(8,128)(2,1)S(1)} %copy-done.4), kind=kOutput, calls=%fused_computation.2 | convolution fusion | flops 2492596224 | bytes 7225344 | tf_op jit(solution)/shard_map/dot_general | solution.py:39
  299.2 4.6 %bitcast_convert_fusion.1.refs_5_ = bf16[1536,768]{1,0:T(8,128)(2,1)} fusion(bf16[2,528,1536]{2,1,0:T(8,128)(2,1)S(1)} %copy-done, bf16[2,528,768]{2,1,0:T(8,128)(2,1)S(1)} %copy-done.5), kind=kOutput, calls=%fused_computation.1 | convolution fusion | flops 2492596224 | bytes 7225344 | tf_op jit(solution)/shard_map/dot_general | solution.py:39
  303.8 90.0 %reduce_all.1 = (f32[2,528,384]{2,1,0:T(8,128)}, f32[2,8,640]{2,1,0:T(8,128)}, f32[8,768]{1,0:T(8,128)}, f32[8,384]{1,0:T(8,128)}, f32[192,768]{1,0:T(8,128)}, /...) custom-call(bf16[2,528,1536]{2,1,0:T(8,128)(2,1)} %get-tuple-element.99.refs_0_, ...), custom_call_target="tpu_custom_call" | custom-call | tf_op jit(solution)/shard_map/reduce_all/pallas_call | solution.py:1481
  395.8 0.9 slice.101
  396.7 1.6 slice.100
  398.3 0.9 slice_multiply_fusion
  399.2 1.3 slice.102
  401.8 1.4 pad_maximum_fusion
  403.3 1.9 copy.37
  405.8 1.4 slice_reduce_fusion.2
  407.3 1.4 slice_bitcast_fusion
  408.7 3.2 fusion.5
  411.9 0.8 copy.45
  (73 shorter events, 12.0 us)
Async XLA Ops:
  7.2 136.0 %all-gather.2.cloned.1.call-start = ((), (), s32[]{:S(2)}) async-start(), calls=%async_computation.1 | async-start | bytes 3932160 | tf_op jit(solution)/shard_map/all_gather | solution.py:1541
  10.7 62.4 %copy-start.11 = (f32[768]{0:T(1024)S(1)}, f32[768]{0:T(1024)}, u32[]{:S(2)}) copy-start(f32[768]{0:T(1024)} %param.29) | copy-start | bytes 9220
  10.7 63.0 %copy-start.12 = (f32[768]{0:T(1024)S(1)}, f32[768]{0:T(1024)}, u32[]{:S(2)}) copy-start(f32[768]{0:T(1024)} %param.23) | copy-start | bytes 9220
  10.7 63.6 %copy-start.13 = (f32[12]{0:T(128)S(1)}, f32[12]{0:T(128)}, u32[]{:S(2)}) copy-start(f32[12]{0:T(128)} %param.28) | copy-start | bytes 148
  73.1 335.5 %reduce-scatter.2.cloned.1.call-start = ((), (), s32[]{:S(2)}) async-start(), calls=%async_computation.2 | async-start | bytes 3932160 | tf_op jit(solution)/shard_map/reduce_scatter | solution.py:1569
  77.0 12.6 %copy-start.16 = (f32[12]{0:T(128)S(1)}, f32[12]{0:T(128)}, u32[]{:S(2)}) copy-start(f32[12]{0:T(128)} %param.27) | copy-start | bytes 148
  77.0 12.7 %copy-start.14 = (f32[12]{0:T(128)S(1)}, f32[12]{0:T(128)}, u32[]{:S(2)}) copy-start(f32[12]{0:T(128)} %param.26) | copy-start | bytes 148
  180.8 1.5 copy-start.9
  265.6 19.1 %copy-start.10 = (f32[8,768]{1,0:T(8,128)S(1)}, f32[8,768]{1,0:T(8,128)}, u32[]{:S(2)}) copy-start(f32[8,768]{1,0:T(8,128)} %get-tuple-element.101) | copy-start | bytes 73732
  265.6 19.8 %copy-start.7 = (bf16[2,528,384]{2,1,0:T(8,128)(2,1)S(1)}, bf16[2,528,384]{2,1,0:T(8,128)(2,1)}, u32[]{:S(2)}) copy-start(bf16[2,528,384]{2,1,0:T(8,128)(2,1)} %get-tuple-element.97.gs_ref) | copy-start | bytes 2433028
  285.3 5.2 %copy-start.3 = (bf16[2,512,1536]{2,1,0:T(8,128)(2,1)S(1)}, bf16[2,512,1536]{2,1,0:T(8,128)(2,1)}, u32[]{:S(2)}) copy-start(bf16[2,512,1536]{2,1,0:T(8,128)(2,1)} %all-gather.2.cloned.1.call-done.cot_ref) | copy-start | bytes 9437188
  285.3 5.2 %copy-start.15 = (bf16[2,512,768]{2,1,0:T(8,128)(2,1)S(1)}, bf16[2,512,768]{2,1,0:T(8,128)(2,1)}, u32[]{:S(2)}) copy-start(bf16[2,512,768]{2,1,0:T(8,128)(2,1)} %get-tuple-element.106) | copy-start | bytes 4718596
  290.6 4.0 copy-start
  290.6 4.0 copy-start.4
  294.6 4.6 %copy-start.5 = (bf16[2,528,768]{2,1,0:T(8,128)(2,1)S(1)}, bf16[2,528,768]{2,1,0:T(8,128)(2,1)}, u32[]{:S(2)}) copy-start(bf16[2,528,768]{2,1,0:T(8,128)(2,1)} %get-tuple-element.96.gx_ref) | copy-start | bytes 4866052
  401.8 6.8 %copy-start.6 = (f32[2,528,384]{2,1,0:T(8,128)S(1)}, f32[2,528,384]{2,1,0:T(8,128)}, u32[]{:S(2)}) copy-start(f32[2,528,384]{2,1,0:T(8,128)} %get-tuple-element.107) | copy-start | bytes 4866052
  403.3 5.4 %copy-start.1 = (bf16[2,512,384]{2,1,0:T(8,128)(2,1)S(1)}, bf16[2,512,384]{2,1,0:T(8,128)(2,1)}, u32[]{:S(2)}) copy-start(bf16[2,512,384]{2,1,0:T(8,128)(2,1)} %x_ref.1) | copy-start | bytes 2359300
  403.3 5.4 %copy-start.2 = (bf16[2,512,384]{2,1,0:T(8,128)(2,1)S(1)}, bf16[2,512,384]{2,1,0:T(8,128)(2,1)}, u32[]{:S(2)}) copy-start(bf16[2,512,384]{2,1,0:T(8,128)(2,1)} %param.16) | copy-start | bytes 2359300
  408.7 3.2 copy-start.8
Sparse Core Ops, SparseCore 0:
  73.2 62.4 all-gather.1
  180.9 62.1 reduce-scatter.1
